TPU v7x, 128 devices: a whole 4x4x4 slice. The times are simulated.
128 devices in a mesh: mesh: 2 (over core), dom: 64 (over z, x, y).
Axes of the slice: x: 4, y: 4, z: 4, core: 2. Of those that a mesh axis runs over, the one named last changes fastest.
Arguments:
- donor_fields: float32 [5, 512, 16384], P(None, None, ('mesh', 'dom')), may hold values from -6 to 6
- interp_weights: float32 [3, 8, 262144], P(None, None, ('mesh', 'dom')), may hold values from -1 to 1, as said below
- donor_owner: int32 [262144, 1], P(('mesh', 'dom')), may hold values from 0 to 63, as said below
- donor_element: int32 [262144], P(('mesh', 'dom')), may hold values from 0 to 127
- geometry: float32 [4, 16384], P(None, ('mesh', 'dom')), may hold values from 0.25 to 4
- wall_flag: int32 [2, 1024], P(None, ('mesh', 'dom')), may hold values 0 or 1
- forcing: float32 [512, 16384], P(None, ('mesh', 'dom')), may hold values from -6 to 6
Outputs:
- velocity: float32 [512, 16384], P(None, ('mesh', 'dom'))
- residual: float32 [512, 16384], P(None, ('mesh', 'dom'))
- interface_values: float32 [5, 262144], P(None, ('mesh', 'dom'))
Inputs may be any that keep to these rules, and one draw needn't show every extreme that they name: `interp_weights`: for each receptor and direction, the 8 entries are the Lagrange polynomials of the order-7 Gauss-Lobatto-Legendre points evaluated at one point of [-1, 1]. `donor_owner`: the receptors of block q of a mesh (the rows of one device) name donor dom indices from q - 2 to q + 2 only; among them one index is named exactly 1024 times and no index more often.
All inputs are finite; a program needn't handle non-finite values. No bound on the sum of `wall_flag` on one device may be relied on, other than what follows from the above.
Results may differ from a plain program's by a relative error of at most 0.00026.
Values sent between devices are 32-bit elements; how exact they have to be, the bound alone decides.
A program may use at most 192 MiB of HBM per device.

v0:
```python
import jax
import jax.numpy as jnp
import numpy as np
from jax import lax
from jax.sharding import PartitionSpec as P

EX = 8
EY = 16
EZ_DEV = 1
ITERS = 3


HIGHEST = lax.Precision.HIGHEST


def with_halo(value, sides, width):
    for axis, dim in sides:
        size, length = (lax.axis_size(axis), value.shape[dim])
        up = [(i, (i + 1) % size) for i in range(size - 1)]
        down = [(j, i) for i, j in up]
        last = lax.slice_in_dim(value, length - width, length, axis=dim)
        leading = lax.slice_in_dim(value, 0, width, axis=dim)
        before = lax.ppermute(last, axis, up)
        after = lax.ppermute(leading, axis, down)
        value = jnp.concatenate([before, value, after], axis=dim)
    return value


def swapped(block, axis, stride):
    count = lax.axis_size(axis)
    route = []
    for low in range(count):
        high = low | 1 << stride
        if high != low and high < count:
            route += [(low, high), (high, low)]
    return lax.ppermute(block, axis, route)


def from_behind(value, axis, steps):
    count = lax.axis_size(axis)
    leading, last = (max(0, -steps), min(count, count - steps))
    return lax.ppermute(value, axis, [(source, source + steps) for source in range(leading, last)])


def from_everyone(value, axis):
    length = lax.axis_size(axis)
    return lax.all_to_all(
        jnp.broadcast_to(value[None], (length, *value.shape)), axis, 0, 0, tiled=True
    )


def taken_together(value, axis):
    return from_everyone(value, axis).sum(axis=0)


def in_one(arrays, axis):
    ends = [0]
    for a in arrays:
        ends.append(ends[-1] + a.size)
    running = taken_together(jnp.concatenate([a.ravel() for a in arrays]), axis)
    return tuple((running[b:e].reshape(a.shape) for a, b, e in zip(arrays, ends, ends[1:])))


def legendre_pair(values, degree):
    previous = values * 0.0 + 1.0
    current = values * 1.0
    for poly_order in range(2, degree + 1):
        previous, current = (
            current,
            ((2 * poly_order - 1) * values * current - (poly_order - 1) * previous) / poly_order,
        )
    return (current, previous)


def gll_tables():
    degree = 7
    points_count = degree + 1
    abscissae = np.cos(np.pi * np.arange(points_count) / degree)
    for newton_turn in range(80):
        top_poly, lower_poly = legendre_pair(abscissae, degree)
        abscissae = abscissae - (abscissae * top_poly - lower_poly) / (points_count * top_poly)
    abscissae = np.sort(abscissae)
    top_poly, lower_poly = legendre_pair(abscissae, degree)
    quad_weights = 2.0 / (degree * points_count * top_poly * top_poly)
    identity_mat = np.eye(points_count)
    spacing = abscissae[:, None] - abscissae[None, :] + identity_mat
    derivative = top_poly[:, None] / (top_poly[None, :] * spacing) * (1.0 - identity_mat)
    derivative[0, 0] = -degree * points_count / 4.0
    derivative[degree, degree] = degree * points_count / 4.0
    return (jnp.asarray(derivative, jnp.float32), jnp.asarray(quad_weights, jnp.float32))


def cube_weights(quad_weights):
    return (
        quad_weights[:, None, None, None]
        * quad_weights[None, :, None, None]
        * quad_weights[None, None, :, None]
    )


def local_operator(field_data, geometry, derivative, quad_weights):
    weights_cube = cube_weights(quad_weights)
    grad_x = jnp.einsum("ai,kjie->kjae", derivative, field_data, precision=HIGHEST)
    grad_y = jnp.einsum("aj,kjie->kaie", derivative, field_data, precision=HIGHEST)
    grad_z = jnp.einsum("ak,kjie->ajie", derivative, field_data, precision=HIGHEST)
    result = jnp.einsum(
        "ai,kjae->kjie", derivative, grad_x * (weights_cube * geometry[0]), precision=HIGHEST
    )
    result = result + jnp.einsum(
        "aj,kaie->kjie", derivative, grad_y * (weights_cube * geometry[1]), precision=HIGHEST
    )
    result = result + jnp.einsum(
        "ak,ajie->kjie", derivative, grad_z * (weights_cube * geometry[2]), precision=HIGHEST
    )
    return result + weights_cube * geometry[3] * field_data


def local_diagonal(geometry, derivative, quad_weights):
    stiff_diag = jnp.sum(derivative * derivative * quad_weights[:, None], axis=0)
    along_x = (
        quad_weights[:, None, None] * quad_weights[None, :, None] * stiff_diag[None, None, :]
    )[..., None]
    along_y = (
        quad_weights[:, None, None] * stiff_diag[None, :, None] * quad_weights[None, None, :]
    )[..., None]
    along_z = (
        stiff_diag[:, None, None] * quad_weights[None, :, None] * quad_weights[None, None, :]
    )[..., None]
    return (
        along_x * geometry[0]
        + along_y * geometry[1]
        + along_z * geometry[2]
        + cube_weights(quad_weights) * geometry[3]
    )


def pair_faces(field_data, axis, stride, has_next):
    has_prev = jnp.roll(has_next, stride)
    low_face = lax.index_in_dim(field_data, 0, axis, keepdims=True)
    high_face = lax.index_in_dim(field_data, 7, axis, keepdims=True)
    next_low = jnp.roll(low_face, -stride, axis=-1)
    prev_high = jnp.roll(high_face, stride, axis=-1)
    new_high = jnp.where(has_next, high_face + next_low, high_face)
    new_low = jnp.where(has_prev, prev_high + low_face, low_face)
    return jnp.concatenate([new_low, lax.slice_in_dim(field_data, 1, 7, axis=axis), new_high], axis)


def direct_sum(field_data):
    elem_count = field_data.shape[-1]
    layer_size = EX * EY
    element_ids = jnp.arange(elem_count, dtype=jnp.int32)
    field_data = pair_faces(field_data, 3, 1, element_ids % EX < EX - 1)
    field_data = pair_faces(field_data, 2, EX, element_ids // EX % EY < EY - 1)
    field_data = pair_faces(field_data, 1, layer_size, element_ids < elem_count - layer_size)
    bottom = field_data[:, 0, :, :, :layer_size]
    top_face = field_data[:, 7, :, :, elem_count - layer_size :]
    face_pair = jnp.stack([bottom, top_face], 0).reshape(2, -1)
    padded = with_halo(face_pair, (("dom", 0),), 1)
    bottom = bottom + padded[0].reshape(bottom.shape)
    top_face = top_face + padded[3].reshape(top_face.shape)
    low_slab = jnp.concatenate([bottom, field_data[:, 0, :, :, layer_size:]], -1)
    high_slab = jnp.concatenate([field_data[:, 7, :, :, : elem_count - layer_size], top_face], -1)
    return jnp.concatenate([low_slab[:, None], field_data[:, 1:7], high_slab[:, None]], 1)


def body(donor_fields, interp_weights, donor_owner, donor_element, geometry, wall_flag, forcing):
    derivative, quad_weights = gll_tables()
    rec_count = donor_element.shape[0]
    elem_count = geometry.shape[1]
    slot_count = rec_count // 2
    field_count = donor_fields.shape[0]
    my_slab = lax.axis_index("dom")
    owner_dom = donor_owner[:, 0]
    distance = owner_dom - my_slab + 2
    onehot = (distance[:, None] == jnp.arange(5, dtype=jnp.int32)[None, :]).astype(jnp.int32)
    position = jnp.sum((jnp.cumsum(onehot, axis=0) - onehot) * onehot, axis=1)
    slot_index = distance * slot_count + position
    source_row = (
        jnp.zeros((5 * slot_count,), jnp.int32)
        .at[slot_index]
        .set(jnp.arange(rec_count, dtype=jnp.int32))
    )
    packed = jnp.concatenate(
        [interp_weights.reshape(24, rec_count), donor_element.astype(jnp.float32)[None, :]], 0
    )
    outgoing = jnp.take(packed, source_row, axis=1)
    crossed = swapped(outgoing, "mesh", 0)
    answers = []
    for slot in range(5):
        piece = crossed[:, slot * slot_count : (slot + 1) * slot_count]
        if slot != 2:
            piece = from_behind(piece, "dom", slot - 2)
        lookups = piece[24].astype(jnp.int32)
        count = lookups.shape[0]
        gathered = jnp.take(donor_fields, lookups, axis=2).reshape(field_count, 64, 8, count)
        reduced = jnp.sum(gathered * piece[0:8][None, None], axis=2).reshape(
            field_count, 8, 8, count
        )
        reduced = jnp.sum(reduced * piece[8:16][None, None], axis=2)
        answers.append(jnp.sum(reduced * piece[16:24][None], axis=1))
    returned = []
    for slot in range(5):
        if slot == 2:
            returned.append(answers[slot])
        else:
            returned.append(from_behind(answers[slot], "dom", 2 - slot))
    answered = swapped(jnp.concatenate(returned, 1), "mesh", 0)
    interface_values = jnp.take(answered, slot_index, axis=1)
    flat_shape = (8, 8, 8, elem_count)
    weights_cube = cube_weights(quad_weights)
    column_count = EZ_DEV * EY
    received = interface_values[0].reshape(2, column_count, 64)
    side_values = jnp.transpose(received, (0, 2, 1)).reshape(2, 8, 8, column_count, 1)
    side_values = jnp.broadcast_to(side_values, (2, 8, 8, column_count, EX)).reshape(
        2, 8, 8, elem_count
    )
    element_ids = jnp.arange(elem_count, dtype=jnp.int32)
    x_index = element_ids % EX
    y_index = element_ids // EX % EY
    z_index = element_ids // (EX * EY)
    node_ids = jnp.arange(8, dtype=jnp.int32)
    low_x = (node_ids[None, None, :, None] == 0) & (x_index[None, None, None, :] == 0)
    high_x = (node_ids[None, None, :, None] == 7) & (x_index[None, None, None, :] == EX - 1)
    rec_value = jnp.where(
        low_x, side_values[0][:, :, None, :], jnp.where(high_x, side_values[1][:, :, None, :], 0.0)
    )
    rec_mark = jnp.where(low_x | high_x, 1.0, 0.0) * jnp.ones(flat_shape, jnp.float32)
    wall_bits = wall_flag.astype(jnp.float32)
    wall_column = z_index * EX + x_index
    wall_low = jnp.take(wall_bits[0], wall_column)
    wall_high = jnp.take(wall_bits[1], wall_column)
    low_y = (node_ids[None, :, None, None] == 0) & (y_index[None, None, None, :] == 0)
    high_y = (node_ids[None, :, None, None] == 7) & (y_index[None, None, None, :] == EY - 1)
    wall_mark = jnp.where(low_y, wall_low, 0.0) + jnp.where(high_y, wall_high, 0.0)
    wall_mark = wall_mark * jnp.ones(flat_shape, jnp.float32)
    diag_local = local_diagonal(geometry, derivative, quad_weights)
    unit_field = jnp.ones(flat_shape, jnp.float32)
    summed = direct_sum(jnp.stack([rec_value, rec_mark, wall_mark, unit_field, diag_local], 0))
    free_mask = 1.0 - jnp.minimum(summed[1] + summed[2], 1.0)
    boundary = summed[0] / jnp.maximum(summed[1], 1.0)
    multiplicity = summed[3]
    inverse = free_mask / summed[4]

    def apply_operator(vector):
        local_term = local_operator(vector, geometry, derivative, quad_weights)
        return free_mask * direct_sum(local_term[None])[0]

    def paired_dots(residual_now, precond, operator_image):
        return in_one(
            (
                jnp.sum(residual_now * precond / multiplicity),
                jnp.sum(precond * operator_image / multiplicity),
            ),
            "dom",
        )

    source = forcing.reshape(flat_shape)
    loaded = weights_cube * geometry[3] * source - local_operator(
        boundary, geometry, derivative, quad_weights
    )
    rhs = free_mask * direct_sum(loaded[None])[0]
    solution = jnp.zeros(flat_shape, jnp.float32)
    residual_now = rhs
    precond = inverse * residual_now
    operator_image = apply_operator(precond)
    precond_norm, curvature = paired_dots(residual_now, precond, operator_image)
    step_length = precond_norm / curvature
    direction = precond
    direction_image = operator_image
    for iteration in range(ITERS):
        solution = solution + step_length * direction
        residual_now = residual_now - step_length * direction_image
        if iteration + 1 < ITERS:
            precond = inverse * residual_now
            operator_image = apply_operator(precond)
            norm_next, curvature = paired_dots(residual_now, precond, operator_image)
            beta_ratio = norm_next / precond_norm
            step_length = norm_next / (curvature - beta_ratio * norm_next / step_length)
            direction = precond + beta_ratio * direction
            direction_image = operator_image + beta_ratio * direction_image
            precond_norm = norm_next
    velocity = (boundary + solution).reshape(-1, elem_count)
    return (velocity, residual_now.reshape(-1, elem_count), interface_values)


def solution(mesh):
    in_specs = (
        P(None, None, ("mesh", "dom")),
        P(None, None, ("mesh", "dom")),
        P(("mesh", "dom"), None),
        P(("mesh", "dom")),
        P(None, ("mesh", "dom")),
        P(None, ("mesh", "dom")),
        P(None, ("mesh", "dom")),
    )
    out_specs = (P(None, ("mesh", "dom")), P(None, ("mesh", "dom")), P(None, ("mesh", "dom")))
    return jax.shard_map(body, mesh=mesh, in_specs=in_specs, out_specs=out_specs, check_vma=False)
```

profile of v0, /device:TPU:0, one launch (start us, length us, event | category | flops | bytes accessed | tf_op | source)
XLA Modules:
  0.0 528.5 jit_solution(16142488344229456810)
XLA Ops:
  4.1 8.1 %scatter_custom_fusion = s32[5120]{0:T(1024)S(1)} fusion(s32[2048]{0:T(1024)S(1)} %bitcast.440, s32[2048]{0:T(1024)S(1)} %iota.92, s32[]{:T(128)} %constant.173.clone.1), kind=kCustom, calls=%fused_computation.310 | custom fusion | bytes 20484 | tf_op jit(solution)/shard_map/scatter | solution.py:181
  14.2 17.7 %gather_fusion = f32[5120,25]{1,0:T(8,128)} fusion(f32[25,2048]{0,1:T(8,128)S(1)} %copy.277, s32[5120]{0:T(1024)S(1)} %fusion.113), kind=kCustom, calls=%fused_computation.5 | custom fusion | bytes 1044480 | tf_op jit(solution)/shard_map/jit(_take)/gather | solution.py:186
  72.8 13.6 %gather_fusion.6 = f32[1024,5,512]{2,1,0:T(8,128)} fusion(f32[5,512,128]{1,0,2:T(8,128)S(1)} %copy.279, s32[1024]{0:T(1024)S(1)} %fusion.120), kind=kCustom, calls=%fused_computation.4.clone | custom fusion | bytes 20975616 | tf_op jit(solution)/shard_map/jit(_take)/gather | solution.py:195
  86.4 12.3 %select_bitcast_fusion = f32[5,512,1024]{1,0,2:T(8,128)} fusion(f32[1024,5,512]{2,1,0:T(8,128)} %gather_fusion.6, pred[1024]{0:T(1024)(128)(4,1)S(1)} %compare_and_fusion.1), kind=kLoop, calls=%fused_computation.8 | loop fusion | flops 2621440 | bytes 20972544 | tf_op jit(solution)/shard_map/jit(_take)/select_n | solution.py:195
  98.7 14.7 %copy.288 = f32[5,512,1024]{2,1,0:T(8,128)} copy(f32[5,512,1024]{1,0,2:T(8,128)} %select_bitcast_fusion) | data formatting | bytes 20971520 | tf_op jit(solution)/shard_map/jit(_take)/select_n | solution.py:195
  113.4 7.8 %fusion = f32[5,64,1024]{2,1,0:T(8,128)S(1)} fusion(f32[5,512,1024]{2,1,0:T(8,128)} %copy.288, f32[8,1024]{1,0:T(8,128)S(1)} %get-tuple-element.93), kind=kLoop, calls=%fused_computation.14 | loop fusion | flops 4915200 | bytes 11829248 | tf_op jit(solution)/shard_map/reduce_sum | solution.py:196
  123.6 13.6 %gather_fusion.5 = f32[1024,5,512]{2,1,0:T(8,128)} fusion(f32[5,512,128]{1,0,2:T(8,128)S(1)} %copy.279, s32[1024]{0:T(1024)S(1)} %get-tuple-element.153), kind=kCustom, calls=%fused_computation.3.clone | custom fusion | bytes 20975616 | tf_op jit(solution)/shard_map/jit(_take)/gather | solution.py:195
  137.2 12.3 %select_bitcast_fusion.1 = f32[5,512,1024]{1,0,2:T(8,128)} fusion(f32[1024,5,512]{2,1,0:T(8,128)} %gather_fusion.5, pred[1024]{0:T(1024)(128)(4,1)S(1)} %compare_and_fusion.2), kind=kLoop, calls=%fused_computation.9 | loop fusion | flops 2621440 | bytes 20972544 | tf_op jit(solution)/shard_map/jit(_take)/select_n | solution.py:195
  149.5 14.7 %copy.286 = f32[5,512,1024]{2,1,0:T(8,128)} copy(f32[5,512,1024]{1,0,2:T(8,128)} %select_bitcast_fusion.1) | data formatting | bytes 20971520 | tf_op jit(solution)/shard_map/jit(_take)/select_n | solution.py:195
  164.1 7.8 %fusion.1 = f32[5,64,1024]{2,1,0:T(8,128)S(1)} fusion(f32[5,512,1024]{2,1,0:T(8,128)} %copy.286, f32[8,1024]{1,0:T(8,128)S(1)} %get-tuple-element.96), kind=kLoop, calls=%fused_computation.16 | loop fusion | flops 4915200 | bytes 11829248 | tf_op jit(solution)/shard_map/reduce_sum | solution.py:196
  173.9 13.6 %gather_fusion.4 = f32[1024,5,512]{2,1,0:T(8,128)} fusion(f32[5,512,128]{1,0,2:T(8,128)S(1)} %copy.279, s32[1024]{0:T(1024)S(1)} %get-tuple-element.152), kind=kCustom, calls=%fused_computation.2.clone | custom fusion | bytes 20975616 | tf_op jit(solution)/shard_map/jit(_take)/gather | solution.py:195
  187.5 12.3 %select_bitcast_fusion.2 = f32[5,512,1024]{1,0,2:T(8,128)} fusion(f32[1024,5,512]{2,1,0:T(8,128)} %gather_fusion.4, pred[1024]{0:T(1024)(128)(4,1)S(1)} %compare_and_fusion.3), kind=kLoop, calls=%fused_computation.10 | loop fusion | flops 2621440 | bytes 20972544 | tf_op jit(solution)/shard_map/jit(_take)/select_n | solution.py:195
  199.8 14.6 %copy.284 = f32[5,512,1024]{2,1,0:T(8,128)} copy(f32[5,512,1024]{1,0,2:T(8,128)} %select_bitcast_fusion.2) | data formatting | bytes 20971520 | tf_op jit(solution)/shard_map/jit(_take)/select_n | solution.py:195
  214.5 13.6 %gather_fusion.3 = f32[1024,5,512]{2,1,0:T(8,128)} fusion(f32[5,512,128]{1,0,2:T(8,128)S(1)} %copy.279, s32[1024]{0:T(1024)S(1)} %get-tuple-element.151), kind=kCustom, calls=%fused_computation.1.clone | custom fusion | bytes 20975616 | tf_op jit(solution)/shard_map/jit(_take)/gather | solution.py:195
  228.1 12.3 %select_bitcast_fusion.3 = f32[5,512,1024]{1,0,2:T(8,128)} fusion(f32[1024,5,512]{2,1,0:T(8,128)} %gather_fusion.3, pred[1024]{0:T(1024)(128)(4,1)S(1)} %compare_and_fusion.4), kind=kLoop, calls=%fused_computation.11 | loop fusion | flops 2621440 | bytes 20972544 | tf_op jit(solution)/shard_map/jit(_take)/select_n | solution.py:195
  240.4 14.7 %copy.282 = f32[5,512,1024]{2,1,0:T(8,128)} copy(f32[5,512,1024]{1,0,2:T(8,128)} %select_bitcast_fusion.3) | data formatting | bytes 20971520 | tf_op jit(solution)/shard_map/jit(_take)/select_n | solution.py:195
  255.1 7.8 %fusion.3 = f32[5,64,1024]{2,1,0:T(8,128)S(1)} fusion(f32[5,512,1024]{2,1,0:T(8,128)} %copy.282, f32[8,1024]{1,0:T(8,128)S(1)} %get-tuple-element.99), kind=kLoop, calls=%fused_computation.20 | loop fusion | flops 4915200 | bytes 11829248 | tf_op jit(solution)/shard_map/reduce_sum | solution.py:196
  268.2 13.6 %gather_fusion.2 = f32[1024,5,512]{2,1,0:T(8,128)} fusion(f32[5,512,128]{1,0,2:T(8,128)S(1)} %copy.279, s32[1024]{0:T(1024)S(1)} %get-tuple-element.150), kind=kCustom, calls=%fused_computation.clone | custom fusion | bytes 20975616 | tf_op jit(solution)/shard_map/jit(_take)/gather | solution.py:195
  281.8 12.3 %select_bitcast_fusion.4 = f32[5,512,1024]{1,0,2:T(8,128)} fusion(f32[1024,5,512]{2,1,0:T(8,128)} %gather_fusion.2, pred[1024]{0:T(1024)(128)(4,1)S(1)} %compare_and_fusion.5), kind=kLoop, calls=%fused_computation.12 | loop fusion | flops 2621440 | bytes 20972544 | tf_op jit(solution)/shard_map/jit(_take)/select_n | solution.py:195
  294.1 14.7 %copy.280 = f32[5,512,1024]{2,1,0:T(8,128)} copy(f32[5,512,1024]{1,0,2:T(8,128)} %select_bitcast_fusion.4) | data formatting | bytes 20971520 | tf_op jit(solution)/shard_map/jit(_take)/select_n | solution.py:195
  399.2 36.9 %all_to_all.18 = f32[64,1,2]{2,1,0:T(1,128)S(1)} all-to-all(f32[64,1,2]{2,1,0:T(1,128)S(1)} %broadcast_in_dim.299), channel_id=1, replica_groups=mesh['mesh'=2,'dom'=64] {'dom'}, dimensions={0} | all-to-all | bytes 1024 | tf_op jit(solution)/shard_map/all_to_all | solution.py:47
  454.7 22.3 %all_to_all.19 = f32[64,1,2]{2,1,0:T(1,128)S(1)} all-to-all(f32[64,1,2]{2,1,0:T(1,128)S(1)} %broadcast_in_dim.301), channel_id=1, replica_groups=mesh['mesh'=2,'dom'=64] {'dom'}, dimensions={0} | all-to-all | bytes 1024 | tf_op jit(solution)/shard_map/all_to_all | solution.py:47
  499.7 12.6 %all-to-all-start.2 = ((f32[64,1,2]{2,1,0:T(1,128)}), f32[64,1,2]{2,1,0:T(1,128)S(1)}, u32[]{:S(2)}, u32[]{:S(2)}) async-start(f32[64,1,2]{2,1,0:T(1,128)} %broadcast_in_dim.303), calls=%async_computation.2 | async-start | bytes 65536 | tf_op jit(solution)/shard_map/all_to_all | solution.py:47
  513.2 8.6 %all-to-all-done.2 = f32[64,1,2]{2,1,0:T(1,128)S(1)} async-done(((f32[64,1,2]{2,1,0:T(1,128)}), f32[64,1,2]{2,1,0:T(1,128)S(1)}, u32[]{:S(2)}, u32[]{:S(2)}) %all-to-all-start.2) | async-done | bytes 544 | tf_op jit(solution)/shard_map/all_to_all | solution.py:47
  (267 shorter events, 184.6 us)
Async XLA Ops:
  37.9 14.6 %collective-permute-start = (f32[25,5120]{1,0:T(8,128)}, f32[25,5120]{1,0:T(8,128)S(1)}, u32[]{:S(2)}, u32[]{:S(2)}) collective-permute-start(f32[25,5120]{1,0:T(8,128)} %copy.278), channel_id=1, source_target_pairs={{0,64},{64,0},{1,65},{65,1},{2,66},{66,2},{3,67},{67,3},{4,68},{68... | collective-permute-start | bytes 1536008 | tf_op jit(solution)/shard_map/ppermute | solution.py:36
  52.6 10.4 %collective-permute-start.7 = (f32[25,1024]{1,0:T(8,128)S(1)}, f32[25,1024]{1,0:T(8,128)S(1)}, u32[]{:S(2)}, u32[]{:S(2)}) collective-permute-start(f32[25,1024]{1,0:T(8,128)S(1)} %get-tuple-element.57), channel_id=1, source_target_pairs={{0,2},{1,3},{2,4},{3,5},{4,6},{5,7},{6,8},{7,9},{8,10},{9,11},{10,... | collective-permute-start | bytes 307208 | tf_op jit(solution)/shard_map/ppermute | solution.py:42
  57.8 6.2 %collective-permute-start.5 = (f32[25,1024]{1,0:T(8,128)S(1)}, f32[25,1024]{1,0:T(8,128)S(1)}, u32[]{:S(2)}, u32[]{:S(2)}) collective-permute-start(f32[25,1024]{1,0:T(8,128)S(1)} %get-tuple-element.58), channel_id=1, source_target_pairs={{0,1},{1,2},{2,3},{3,4},{4,5},{5,6},{6,7},{7,8},{8,9},{9,10},{10,1... | collective-permute-start | bytes 307208 | tf_op jit(solution)/shard_map/ppermute | solution.py:42
  60.4 7.2 %collective-permute-start.3 = (f32[25,1024]{1,0:T(8,128)S(1)}, f32[25,1024]{1,0:T(8,128)S(1)}, u32[]{:S(2)}, u32[]{:S(2)}) collective-permute-start(f32[25,1024]{1,0:T(8,128)S(1)} %get-tuple-element.59), channel_id=1, source_target_pairs={{1,0},{2,1},{3,2},{4,3},{5,4},{6,5},{7,6},{8,7},{9,8},{10,9},{11,1... | collective-permute-start | bytes 307208 | tf_op jit(solution)/shard_map/ppermute | solution.py:42
  61.7 11.1 %collective-permute-start.1 = (f32[25,1024]{1,0:T(8,128)S(1)}, f32[25,1024]{1,0:T(8,128)S(1)}, u32[]{:S(2)}, u32[]{:S(2)}) collective-permute-start(f32[25,1024]{1,0:T(8,128)S(1)} %get-tuple-element.60), channel_id=1, source_target_pairs={{2,0},{3,1},{4,2},{5,3},{6,4},{7,5},{8,6},{9,7},{10,8},{11,9},{12,... | collective-permute-start | bytes 307208 | tf_op jit(solution)/shard_map/ppermute | solution.py:42
  121.7 209.8 %collective-permute-start.8 = (f32[5,1024]{1,0:T(8,128)S(1)}, f32[5,1024]{1,0:T(8,128)S(1)}, u32[]{:S(2)}, u32[]{:S(2)}) collective-permute-start(f32[5,1024]{1,0:T(8,128)S(1)} %multiply_reduce_fusion), channel_id=1, source_target_pairs={{2,0},{3,1},{4,2},{5,3},{6,4},{7,5},{8,6},{9,7},{10,8},{11,9},{12,... | collective-permute-start | bytes 61448 | tf_op jit(solution)/shard_map/ppermute | solution.py:42
  172.5 159.1 %collective-permute-start.6 = (f32[5,1024]{1,0:T(8,128)S(1)}, f32[5,1024]{1,0:T(8,128)S(1)}, u32[]{:S(2)}, u32[]{:S(2)}) collective-permute-start(f32[5,1024]{1,0:T(8,128)S(1)} %multiply_reduce_fusion.1), channel_id=1, source_target_pairs={{1,0},{2,1},{3,2},{4,3},{5,4},{6,5},{7,6},{8,7},{9,8},{10,9},{11,1... | collective-permute-start | bytes 61448 | tf_op jit(solution)/shard_map/ppermute | solution.py:42
  263.4 68.1 %collective-permute-start.4 = (f32[5,1024]{1,0:T(8,128)S(1)}, f32[5,1024]{1,0:T(8,128)S(1)}, u32[]{:S(2)}, u32[]{:S(2)}) collective-permute-start(f32[5,1024]{1,0:T(8,128)S(1)} %multiply_reduce_fusion.3), channel_id=1, source_target_pairs={{0,1},{1,2},{2,3},{3,4},{4,5},{5,6},{6,7},{7,8},{8,9},{9,10},{10,1... | collective-permute-start | bytes 61448 | tf_op jit(solution)/shard_map/ppermute | solution.py:42
  317.1 14.4 %collective-permute-start.2 = (f32[5,1024]{1,0:T(8,128)S(1)}, f32[5,1024]{1,0:T(8,128)S(1)}, u32[]{:S(2)}, u32[]{:S(2)}) collective-permute-start(f32[5,1024]{1,0:T(8,128)S(1)} %multiply_reduce_fusion.4), channel_id=1, source_target_pairs={{0,2},{1,3},{2,4},{3,5},{4,6},{5,7},{6,8},{7,9},{8,10},{9,11},{10,... | collective-permute-start | bytes 61448 | tf_op jit(solution)/shard_map/ppermute | solution.py:42
  331.6 1.9 collective-permute-start.9
  348.6 8.6 %collective-permute-start.10 = (f32[1,40960]{1,0:T(1,128)S(1)}, f32[1,40960]{1,0:T(1,128)S(1)}, u32[]{:S(2)}, u32[]{:S(2)}) collective-permute-start(f32[1,40960]{1,0:T(1,128)S(1)} %bitcast.409), channel_id=1, source_target_pairs={{0,1},{1,2},{2,3},{3,4},{4,5},{5,6},{6,7},{7,8},{8,9},{9,10},{10,1... | collective-permute-start | bytes 491528 | tf_op jit(solution)/shard_map/ppermute | solution.py:23
  357.3 8.0 %collective-permute-start.11 = (f32[1,40960]{1,0:T(1,128)S(1)}, f32[1,40960]{1,0:T(1,128)S(1)}, u32[]{:S(2)}, u32[]{:S(2)}) collective-permute-start(f32[1,40960]{1,0:T(1,128)S(1)} %bitcast.412), channel_id=1, source_target_pairs={{1,0},{2,1},{3,2},{4,3},{5,4},{6,5},{7,6},{8,7},{9,8},{10,9},{11,1... | collective-permute-start | bytes 491528 | tf_op jit(solution)/shard_map/ppermute | solution.py:24
  369.8 5.2 collective-permute-start.12
  375.0 6.1 %collective-permute-start.13 = (f32[1,8192]{1,0:T(1,128)S(1)}, f32[1,8192]{1,0:T(1,128)S(1)}, u32[]{:S(2)}, u32[]{:S(2)}) collective-permute-start(f32[1,8192]{1,0:T(1,128)S(1)} %bitcast.442), channel_id=1, source_target_pairs={{1,0},{2,1},{3,2},{4,3},{5,4},{6,5},{7,6},{8,7},{9,8},{10,9},{11,1... | collective-permute-start | bytes 98312 | tf_op jit(solution)/shard_map/ppermute | solution.py:24
  381.2 100.7 %copy-start.2 = (f32[1,8,8,8,128]{4,3,2,1,0:T(8,128)}, f32[1,8,8,8,128]{4,3,2,1,0:T(8,128)S(1)}, u32[]{:S(2)}) copy-start(f32[1,8,8,8,128]{4,3,2,1,0:T(8,128)S(1)} %get-tuple-element.41) | copy-start | bytes 786436
  384.9 6.0 %collective-permute-start.14 = (f32[1,8192]{1,0:T(1,128)S(1)}, f32[1,8192]{1,0:T(1,128)S(1)}, u32[]{:S(2)}, u32[]{:S(2)}) collective-permute-start(f32[1,8192]{1,0:T(1,128)S(1)} %bitcast.416), channel_id=1, source_target_pairs={{0,1},{1,2},{2,3},{3,4},{4,5},{5,6},{6,7},{7,8},{8,9},{9,10},{10,1... | collective-permute-start | bytes 98312 | tf_op jit(solution)/shard_map/ppermute | solution.py:23
  391.0 6.1 %collective-permute-start.15 = (f32[1,8192]{1,0:T(1,128)S(1)}, f32[1,8192]{1,0:T(1,128)S(1)}, u32[]{:S(2)}, u32[]{:S(2)}) collective-permute-start(f32[1,8192]{1,0:T(1,128)S(1)} %bitcast.443), channel_id=1, source_target_pairs={{1,0},{2,1},{3,2},{4,3},{5,4},{6,5},{7,6},{8,7},{9,8},{10,9},{11,1... | collective-permute-start | bytes 98312 | tf_op jit(solution)/shard_map/ppermute | solution.py:24
  441.8 4.1 collective-permute-start.16
  445.9 6.1 %collective-permute-start.17 = (f32[1,8192]{1,0:T(1,128)S(1)}, f32[1,8192]{1,0:T(1,128)S(1)}, u32[]{:S(2)}, u32[]{:S(2)}) collective-permute-start(f32[1,8192]{1,0:T(1,128)S(1)} %bitcast.444), channel_id=1, source_target_pairs={{1,0},{2,1},{3,2},{4,3},{5,4},{6,5},{7,6},{8,7},{9,8},{10,9},{11,1... | collective-permute-start | bytes 98312 | tf_op jit(solution)/shard_map/ppermute | solution.py:24
  486.7 4.0 collective-permute-start.18
  490.7 6.1 %collective-permute-start.19 = (f32[1,8192]{1,0:T(1,128)S(1)}, f32[1,8192]{1,0:T(1,128)S(1)}, u32[]{:S(2)}, u32[]{:S(2)}) collective-permute-start(f32[1,8192]{1,0:T(1,128)S(1)} %bitcast.445), channel_id=1, source_target_pairs={{1,0},{2,1},{3,2},{4,3},{5,4},{6,5},{7,6},{8,7},{9,8},{10,9},{11,1... | collective-permute-start | bytes 98312 | tf_op jit(solution)/shard_map/ppermute | solution.py:24
  497.7 29.7 %copy-start.1 = (f32[1,8,8,8,128]{4,3,2,1,0:T(8,128)S(1)}, f32[1,8,8,8,128]{4,3,2,1,0:T(8,128)}, u32[]{:S(2)}) copy-start(f32[1,8,8,8,128]{4,3,2,1,0:T(8,128)} %copy-done) | copy-start | bytes 786436
  497.7 29.7 %copy-start.3 = (f32[1,8,8,8,128]{4,3,2,1,0:T(8,128)S(1)}, f32[1,8,8,8,128]{4,3,2,1,0:T(8,128)}, u32[]{:S(2)}) copy-start(f32[1,8,8,8,128]{4,3,2,1,0:T(8,128)} %copy-done.2) | copy-start | bytes 786436
  499.7 22.2 %all-to-all-start.2 = ((f32[64,1,2]{2,1,0:T(1,128)}), f32[64,1,2]{2,1,0:T(1,128)S(1)}, u32[]{:S(2)}, u32[]{:S(2)}) async-start(f32[64,1,2]{2,1,0:T(1,128)} %broadcast_in_dim.303), calls=%async_computation.2 | async-start | bytes 65536 | tf_op jit(solution)/shard_map/all_to_all | solution.py:47
  (11 other events, 66.4 us)
where the time goes:
time: 539 us; the launch traced here: 529 us
  local copies, waits for them, and re-layouts  189 us (35%)
  other arithmetic  141 us (26%)
  starting transfers between devices  62.1 us (12%)
  blocking collectives  59.2 us (11%)
  waiting for transfers between devices  55.5 us (10%)
  between operations  11.5 us (2%)
  matrix products  10.3 us (2%)
    select_n x5, local copies, waits for them, and re-layouts, body(): jnp.take(donor_fields, lookups, axis=2).reshape(field_count, 64, 8, count)  73.3 us
    gather x5, local copies, waits for them, and re-layouts, body(): jnp.take(donor_fields, lookups, axis=2).reshape(field_count, 64, 8, count)  68 us
    select_n x5, other arithmetic, body(): jnp.take(donor_fields, lookups, axis=2).reshape(field_count, 64, 8, count)  61.5 us
    all_to_all x2, blocking collectives, from_everyone(): lax.all_to_all(jnp.broadcast_to(value[None], (length, *value.shape)), axi...  59.2 us
    reduce_sum x5, other arithmetic, body(): jnp.sum(gathered * piece[0:8][None, None], axis=2)  39.1 us
    ppermute x5, waiting for transfers between devices, with_halo(): after = lax.ppermute(leading, axis, down)  25.8 us
    ppermute x8, starting transfers between devices, from_behind(): lax.ppermute(value, axis, [(source, source + steps) for source in range(l...  24.5 us
    ppermute x5, starting transfers between devices, with_halo(): before = lax.ppermute(last, axis, up)  17.9 us
  transfers between devices with their start and end apart: 21, of which 15 were waited for; matrix products, arithmetic and copies ran while one was open for 40% of the time, Pallas kernels for 0%

commit v1 on v0

v1 whole, which is shorter than its diff:
```python
import functools

import jax
import jax.numpy as jnp
import numpy as np
from jax import lax
from jax.experimental import pallas as pl
from jax.experimental.pallas import tpu as pltpu
from jax.sharding import PartitionSpec as P

MESH = pl.DeviceIdType.MESH
F32 = jnp.float32
NQ = 64
NB = 80


def legendre_pair(values, degree):
    previous = values * 0.0 + 1.0
    current = values * 1.0
    for order in range(2, degree + 1):
        previous, current = (
            current,
            ((2 * order - 1) * values * current - (order - 1) * previous) / order,
        )
    return current, previous


def gll():
    degree, count = 7, 8
    x = np.cos(np.pi * np.arange(count) / degree)
    for _ in range(80):
        top, lower = legendre_pair(x, degree)
        x = x - (x * top - lower) / (count * top)
    x = np.sort(x)
    top, _ = legendre_pair(x, degree)
    w = 2.0 / (degree * count * top * top)
    eye = np.eye(count)
    d = top[:, None] / (top[None, :] * (x[:, None] - x[None, :] + eye)) * (1.0 - eye)
    d[0, 0] = -degree * count / 4.0
    d[7, 7] = degree * count / 4.0
    return x, w, d


X, WQ, D = gll()
KP = (D.T * WQ[None, :]) @ D / WQ[:, None]
KP = 0.5 * (KP + KP[::-1, ::-1])
KE = 0.5 * (KP[:4, :4] + KP[:4, 7:3:-1])
KO = 0.5 * (KP[:4, :4] - KP[:4, 7:3:-1])
LC = np.array([1.0 / np.prod([X[n] - X[m] for m in range(8) if m != n]) for n in range(8)])


def const_table():
    lane = np.arange(128)
    xl = lane % 8
    rows = []
    rows.append(np.repeat(X[:, None], 128, 1))
    rows.append(np.repeat(WQ[:, None], 128, 1))
    for s in range(8):
        rows.append(np.repeat(np.array([KP[i, (i + s) % 8] for i in range(8)])[:, None], 128, 1))
    kx = np.zeros((8, 128))
    for i in range(8):
        kx[i] = np.where(xl == 0, KP[i, 0], np.where(xl == 7, KP[i, 7], 0.0))
    kx[0] = np.where(xl == 1, KP[7, 0], kx[0])
    kx[7] = np.where(xl == 6, KP[0, 7], kx[7])
    rows.append(kx)
    rows.append((np.arange(8)[:, None] == xl[None, :]).astype(float))
    return np.concatenate(rows, 0).astype(np.float32)


def kernel(
    donor_hbm, wts, owner, elem, geo, wall, forc_hbm, ct,
    vel, res, iv,
    donor, forc, req_src, req, aux_src, aux, W, IDX, ans_src, ans,
    FB, OUT, R0, INV, V, WA, DG, ND, QB, face_src, face, halo, ar,
    in_sem, req_s, req_r, aux_s, aux_r, ans_s, ans_r, face_s, face_r, halo_s, halo_r, ar_s, ar_r,
):
    m = lax.axis_index("mesh")
    q = lax.axis_index("dom")
    om = 1 - m
    barrier = pltpu.get_barrier_semaphore()

    def there(d):
        return jnp.logical_and(q + d >= 0, q + d < NQ)

    for d, s in ((-1, 0), (1, 1)):
        @pl.when(jnp.logical_not(there(d)))
        def _(s=s):
            aux[s] = jnp.zeros((8, 128), F32)
            face[s] = jnp.zeros((8, 128), F32)
            for r in range(4):
                halo[r, s] = jnp.zeros((64, 128), F32)
    for d in (-2, -1, 1, 2):
        @pl.when(jnp.logical_not(there(d)))
        def _(d=d):
            req[2 - d] = jnp.zeros((64, 128), F32)
            ans[2 + d] = jnp.zeros((5, 16, 128), F32)

    in_donor = pltpu.make_async_copy(donor_hbm, donor, in_sem.at[0])
    in_forc = pltpu.make_async_copy(forc_hbm, forc, in_sem.at[1])
    in_forc.start()
    in_donor.start()

    def greet(d, c):
        peer = lax.rem(q + d, NQ)
        pl.semaphore_signal(barrier, inc=1, device_id=(m, peer), device_id_type=MESH)
        return c

    lax.fori_loop(1, NQ, greet, 0)
    for d in range(-2, 3):
        @pl.when(there(d))
        def _(d=d):
            pl.semaphore_signal(barrier, inc=1, device_id=(om, q + d), device_id_type=MESH)

    i0 = lax.broadcasted_iota(jnp.int32, (8, 128), 0)
    lane = lax.broadcasted_iota(jnp.int32, (8, 128), 1)
    xl = lane & 7
    yl = lane >> 3
    xcol = ct[0:8, :]
    wcol = ct[8:16, :]

    for d in range(3):
        for b in range(16):
            t = wts[d, :, b * 128 : (b + 1) * 128] * xcol
            req_src[d * 16 + b : d * 16 + b + 1, :] = jnp.sum(t, axis=0, keepdims=True)
    req_src[48:64, :] = (owner[...] * 128 + elem[...]).astype(F32)
    aux_src[0:4, :] = geo[...]
    aux_src[4:6, :] = jnp.dot(
        wall[...].astype(F32), ct[88:96, :], preferred_element_type=F32
    )
    aux_src[6:8, :] = jnp.zeros((2, 128), F32)

    width = sum(there(d).astype(jnp.int32) for d in range(-2, 3))
    pl.semaphore_wait(barrier, NQ - 1 + width)

    def req_copy(d):
        return pltpu.make_async_remote_copy(
            req_src, req.at[d + 2], req_s.at[d + 2], req_r.at[d + 2],
            device_id=(om, q + d), device_id_type=MESH)

    def aux_copy(d):
        s = (d + 1) // 2
        return pltpu.make_async_remote_copy(
            aux_src, aux.at[1 - s], aux_s.at[s], aux_r.at[1 - s],
            device_id=(m, q + d), device_id_type=MESH)

    def face_copy(d):
        s = (d + 1) // 2
        return pltpu.make_async_remote_copy(
            face_src.at[s], face.at[1 - s], face_s.at[s], face_r.at[1 - s],
            device_id=(m, q + d), device_id_type=MESH)

    def halo_copy(src, r, d):
        s = (d + 1) // 2
        return pltpu.make_async_remote_copy(
            src.at[pl.ds(s * 448, 64)], halo.at[r, 1 - s], halo_s.at[r, s], halo_r.at[r, 1 - s],
            device_id=(m, q + d), device_id_type=MESH)

    def ans_copy(f, s):
        d = 2 - s
        return pltpu.make_async_remote_copy(
            ans_src.at[f, pl.ds(s * 16, 16)], ans.at[s, f], ans_s.at[f, s], ans_r.at[f, s],
            device_id=(om, q + d), device_id_type=MESH)

    def when_there(d, act):
        @pl.when(there(d))
        def _():
            act()

    for d in (2, -2, 1, -1, 0):
        when_there(d, lambda d=d: req_copy(d).start())
    for d in (-1, 1):
        when_there(d, lambda d=d: aux_copy(d).start())

    m7x = jnp.logical_and(i0 == 7, xl < 7)
    m0x = jnp.logical_and(i0 == 0, xl > 0)
    m7y = jnp.logical_and(i0 == 7, yl < 15)
    m0y = jnp.logical_and(i0 == 0, yl > 0)
    xhi, xlo = xl < 7, xl > 0
    yhi, ylo = yl < 15, yl > 0

    def sum_xy(ref, base, planes):
        for k in range(planes):
            lo = ref[pl.ds(base + k * 64, 8, stride=8), :]
            hi = ref[pl.ds(base + k * 64 + 7, 8, stride=8), :]
            ref[pl.ds(base + k * 64, 8, stride=8), :] = lo + jnp.where(
                xlo, pltpu.roll(hi, 1, axis=1), 0.0)
            ref[pl.ds(base + k * 64 + 7, 8, stride=8), :] = hi + jnp.where(
                xhi, pltpu.roll(lo, 127, axis=1), 0.0)
        for k in range(planes):
            at = base + k * 64
            lo = ref[at : at + 8, :]
            hi = ref[at + 56 : at + 64, :]
            ref[at : at + 8, :] = lo + jnp.where(ylo, pltpu.roll(hi, 8, axis=1), 0.0)
            ref[at + 56 : at + 64, :] = hi + jnp.where(yhi, pltpu.roll(lo, 120, axis=1), 0.0)

    def rows(ref, n):
        return jnp.broadcast_to(ref[n : n + 1, :], (8, 128))

    g0, g1, g2, g3 = (rows(geo, n) for n in range(4))

    def tile(k, j):
        at = (k * 8 + j) * 8
        return slice(at, at + 8)

    def wkj(k, j):
        return float(WQ[k] * WQ[j])

    in_forc.wait()
    g3w = g3 * wcol
    for k in range(8):
        for j in range(8):
            FB[tile(k, j), :] = forc[tile(k, j), :] * (g3w * wkj(k, j))
    sum_xy(FB, 0, 8)
    for d in (-1, 1):
        when_there(d, lambda d=d: halo_copy(FB, 0, d).start())

    for d, s in ((-1, 0), (1, 1)):
        when_there(d, lambda d=d, s=s: aux_copy(-d).wait_recv())

    plane = jnp.logical_or(
        jnp.logical_and(i0 == 0, xl == 0), jnp.logical_and(i0 == 7, xl == 7))
    pm = jnp.where(plane, 0.0, 1.0)

    def wall_count(row):
        return (row + jnp.where(m7x, pltpu.roll(row, 127, axis=1), 0.0)
                + jnp.where(m0x, pltpu.roll(row, 1, axis=1), 0.0))

    masks = {}
    for n, (j, edge) in enumerate(((0, yl == 0), (7, yl == 15))):
        own = wall_count(rows(aux_src, 4 + n))
        below = wall_count(jnp.broadcast_to(aux[0, 4 + n : 5 + n, :], (8, 128)))
        above = wall_count(jnp.broadcast_to(aux[1, 4 + n : 5 + n, :], (8, 128)))
        for name, count in (("lo", own + below), ("in", own), ("hi", own + above)):
            masks[j, name] = pm * (1.0 - jnp.where(edge, jnp.minimum(count, 1.0), 0.0))

    def free(k, j):
        if j not in (0, 7):
            return pm
        return masks[j, "lo" if k == 0 else "hi" if k == 7 else "in"]

    kdiag = ct[16:24, :]

    def diag_tile(h0, h1, h2, h3, k, j):
        return (h0 * kdiag + h1 * float(KP[j, j]) + h2 * float(KP[k, k]) + h3) * (
            wcol * wkj(k, j))

    for k in range(8):
        for j in range(8):
            DG[tile(k, j), :] = diag_tile(g0, g1, g2, g3, k, j)
    for s in range(2):
        h = [jnp.broadcast_to(aux[s, n : n + 1, :], (8, 128)) for n in range(4)]
        for j in range(8):
            ND[s * 64 + j * 8 : s * 64 + j * 8 + 8, :] = diag_tile(*h, 0, j)
    sum_xy(DG, 0, 8)
    sum_xy(ND, 0, 2)
    for k in range(8):
        for j in range(8):
            value = DG[tile(k, j), :]
            if k == 0:
                value = value + ND[tile(0, j), :]
            if k == 7:
                value = value + ND[tile(1, j), :]
            INV[tile(k, j), :] = free(k, j) / value

    in_donor.wait()

    def weights(s):
        for h in range(2):
            at = s * 16 + 8 * h
            code = req[s, 48 + 8 * h : 56 + 8 * h, :] - (q * 128).astype(F32)
            mine = jnp.logical_and(code >= 0.0, code < 128.0)
            IDX[at : at + 8, :] = jnp.where(mine, code, 0.0).astype(jnp.int32)
            keep = jnp.where(mine, 1.0, 0.0)
            for d in range(3):
                xi = req[s, d * 16 + 8 * h : d * 16 + 8 * h + 8, :]
                t = [xi - float(X[n]) for n in range(8)]
                pre, suf = [None], [None] * 8
                for n in range(1, 8):
                    pre.append(t[n - 1] if n == 1 else pre[-1] * t[n - 1])
                for n in range(6, -1, -1):
                    suf[n] = t[7] if n == 6 else suf[n + 1] * t[n + 1]
                for n in range(8):
                    a = suf[0] if n == 0 else pre[7] if n == 7 else pre[n] * suf[n]
                    a = a * float(LC[n])
                    if d == 0:
                        a = a * keep
                    W[(d * 8 + n) * NB + at : (d * 8 + n) * NB + at + 8, :] = a

    def evaluate(f, first, count, unroll):
        def block(b):
            idx = jnp.broadcast_to(IDX[pl.ds(b, 1), :], (8, 128))
            wi = W[pl.ds(b, 8, stride=NB), :]
            total = None
            for k in range(8):
                wk = jnp.broadcast_to(W[pl.ds((16 + k) * NB + b, 1), :], (8, 128))
                part = None
                for j in range(8):
                    wj = jnp.broadcast_to(W[pl.ds((8 + j) * NB + b, 1), :], (8, 128))
                    g = jnp.take_along_axis(
                        donor[f, tile(k, j), :], idx, axis=1, mode="promise_in_bounds")
                    part = g * wj if part is None else part + g * wj
                total = part * wk if total is None else total + part * wk
            ans_src[f, pl.ds(b, 1), :] = jnp.sum(total * wi, axis=0, keepdims=True)

        def step(n, c):
            for u in range(unroll):
                block(first + n * unroll + u)
            return c

        lax.fori_loop(0, count // unroll, step, 0)

    def send_field(f):
        for s in (0, 4, 1, 3, 2):
            when_there(2 - s, lambda s=s: ans_copy(f, s).start())

    for s in (2, 1, 3, 0, 4):
        when_there(2 - s, lambda s=s: req_copy(s - 2).wait_recv())
        weights(s)
        evaluate(0, s * 16, 16, 8)
        when_there(2 - s, lambda s=s: ans_copy(0, s).start())

    evaluate(1, 0, NB, 8)
    send_field(1)

    for s in range(5):
        when_there(s - 2, lambda s=s: ans_copy(0, s).wait_recv())
    got = ans[0, 0] + ans[1, 0] + ans[2, 0] + ans[3, 0] + ans[4, 0]
    turned = jnp.transpose(jnp.concatenate([got, jnp.zeros((112, 128), F32)], 0))
    column = jnp.where(xl == 7, 8, 0) + (yl >> 1)
    even = (yl & 1) == 0
    ends = jnp.logical_or(xl == 0, xl == 7)
    T = []
    for k in range(8):
        a = jnp.take_along_axis(turned[k * 8 : k * 8 + 8, :], column, axis=1,
                                mode="promise_in_bounds")
        b = jnp.take_along_axis(turned[64 + k * 8 : 72 + k * 8, :], column, axis=1,
                                mode="promise_in_bounds")
        t = jnp.where(ends, jnp.where(even, a, b), 0.0)
        T.append(t + jnp.where(m7y, pltpu.roll(pltpu.roll(t, 120, axis=1), 7, axis=0), 0.0)
                 + jnp.where(m0y, pltpu.roll(pltpu.roll(t, 8, axis=1), 1, axis=0), 0.0))
    face_src[0] = T[0]
    face_src[1] = T[7]
    for d in (-1, 1):
        when_there(d, lambda d=d: face_copy(d).start())

    evaluate(2, 0, NB, 8)
    send_field(2)

    for d in (-1, 1):
        when_there(d, lambda d=d: face_copy(-d).wait_recv())
    T[0] = T[0] + face[0]
    T[7] = T[7] + face[1]
    czd = jnp.where(q > 0, 0.5, 1.0).astype(F32)
    czu = jnp.where(q < NQ - 1, 0.5, 1.0).astype(F32)
    cyv = jnp.where(jnp.logical_or(m7y, m0y), 0.5, 1.0)

    def spread_y(row):
        return (row + jnp.where(m7y, pltpu.roll(row, 120, axis=1), 0.0)
                + jnp.where(m0y, pltpu.roll(row, 8, axis=1), 0.0))

    gy = spread_y(g0)
    gy_below = spread_y(jnp.broadcast_to(aux[0, 0:1, :], (8, 128)))
    gy_above = spread_y(jnp.broadcast_to(aux[1, 0:1, :], (8, 128)))
    for k in range(8):
        b = T[k] * cyv
        gs = gy
        if k == 0:
            b, gs = b * czd, gs + gy_below
        if k == 7:
            b, gs = b * czu, gs + gy_above
        QB[64 + k * 8 : 72 + k * 8, :] = b
        t = b * gs
        t = jnp.where(xl == 1, pltpu.roll(t, 1, axis=1),
                      jnp.where(xl == 6, pltpu.roll(t, 127, axis=1), t))
        QB[k * 8 : k * 8 + 8, :] = t

    cx = jnp.where(jnp.logical_or(m7x, m0x), 0.5, 1.0)
    cxy = {0: cx * jnp.where(ylo, 0.5, 1.0), 7: cx * jnp.where(yhi, 0.5, 1.0)}

    def assembled(src, r, k, j):
        value = src[tile(k, j), :]
        if k == 0:
            value = value + halo[r, 0, j * 8 : j * 8 + 8, :]
        if k == 7:
            value = value + halo[r, 1, j * 8 : j * 8 + 8, :]
        return value

    def wait_halo(src, r):
        for d in (-1, 1):
            when_there(d, lambda d=d: halo_copy(src, r, -d).wait_recv())

    def product_sum(make):
        total = None
        for k in range(8):
            part = None
            for j in range(8):
                t = make(k, j) * cxy.get(j, cx)
                part = t if part is None else part + t
            if k == 0:
                part = part * czd
            if k == 7:
                part = part * czu
            total = part if total is None else total + part
        return total

    kxw = ct[80:88, :] * wcol
    wait_halo(FB, 0)

    def first(k, j):
        value = assembled(FB, 0, k, j) - rows(QB, k * 8 + j) * (kxw * wkj(k, j))
        value = value * free(k, j)
        R0[tile(k, j), :] = value
        pre = value * INV[tile(k, j), :]
        V[0, tile(k, j), :] = pre
        return value * pre

    moments = [product_sum(first)]

    kroll = [ct[16 + 8 * s : 24 + 8 * s, :] for s in range(8)]

    def eight(v):
        e = [v[n] + v[7 - n] for n in range(4)]
        o = [v[n] - v[7 - n] for n in range(4)]
        out = [None] * 8
        for n in range(4):
            a, b = None, None
            for c in range(4):
                ta, tb = e[c] * float(KE[n, c]), o[c] * float(KO[n, c])
                a = ta if a is None else a + ta
                b = tb if b is None else b + tb
            out[n], out[7 - n] = a + b, a - b
        return out

    def local_operator(src, dst):
        for j in range(8):
            v = [src[tile(k, j), :] for k in range(8)]
            z = eight(v)
            for k in range(8):
                dst[tile(k, j), :] = z[k] * g2 + v[k] * g3
        energy = None
        for k in range(8):
            v = [src[tile(k, j), :] for j in range(8)]
            y = eight(v)
            for j in range(8):
                x = v[j] * kroll[0]
                for s in range(1, 8):
                    x = x + pltpu.roll(v[j], 8 - s, axis=0) * kroll[s]
                value = (dst[tile(k, j), :] + y[j] * g1 + x * g0) * (wcol * wkj(k, j))
                dst[tile(k, j), :] = value
                t = v[j] * value
                energy = t if energy is None else energy + t
        return energy

    def fold(n):
        def make(k, j):
            value = assembled(OUT, n + 1, k, j) * free(k, j)
            WA[n, tile(k, j), :] = value
            pre = value * INV[tile(k, j), :]
            if n < 2:
                V[n + 1, tile(k, j), :] = pre
            return value * pre

        return product_sum(make)

    for n in range(3):
        moments.append(local_operator(V.at[n], OUT))
        if n == 2:
            row = jnp.zeros((1, 128), F32)
            one = lax.broadcasted_iota(jnp.int32, (1, 128), 1)
            for at, t in enumerate(moments):
                t = jnp.sum(jnp.sum(t, axis=0, keepdims=True), axis=1, keepdims=True)
                row = jnp.where(one == at, t, row)
            ar[q] = row

            def tell(d, c):
                peer = lax.rem(q + d, NQ)
                pltpu.make_async_remote_copy(
                    ar.at[q], ar.at[q], ar_s.at[d], ar_r.at[q],
                    device_id=(m, peer), device_id_type=MESH).start()
                return c

            lax.fori_loop(1, NQ, tell, 0)
        sum_xy(OUT, 0, 8)
        for d in (-1, 1):
            when_there(d, lambda d=d: halo_copy(OUT, n + 1, d).start())
        if n < 2:
            evaluate(3 + n, 0, NB, 8)
            send_field(3 + n)
        wait_halo(OUT, n + 1)
        if n < 2:
            for d in (-1, 1):
                when_there(d, lambda d=d: halo_copy(OUT, n + 1, d).wait_send())
            moments.append(fold(n))
        else:
            fold(n)

    for f in range(1, 5):
        for s in range(5):
            when_there(s - 2, lambda f=f, s=s: ans_copy(f, s).wait_recv())
    for f in range(5):
        t = ans[0, f] + ans[1, f] + ans[2, f] + ans[3, f] + ans[4, f]
        for b in range(16):
            iv[f : f + 1, b * 128 : (b + 1) * 128] = t[b : b + 1, :]

    def hear(d, c):
        peer = lax.rem(q + d, NQ)
        pltpu.make_async_remote_copy(
            ar.at[peer], ar.at[peer], ar_s.at[d], ar_r.at[peer],
            device_id=(m, peer), device_id_type=MESH).wait_recv()
        return c

    lax.fori_loop(1, NQ, hear, 0)
    parts = [ar[n] for n in range(NQ)]
    while len(parts) > 1:
        parts = [parts[n] + parts[n + 1] for n in range(0, len(parts), 2)]
    sums = jnp.broadcast_to(parts[0], (8, 128))
    mu = [
        jnp.take_along_axis(sums, jnp.full((8, 128), n, jnp.int32), axis=1,
                            mode="promise_in_bounds")
        for n in range(6)
    ]

    def quad(c, shift):
        total = None
        for a in range(len(c)):
            for b in range(a, len(c)):
                t = c[a] * c[b] * mu[a + b + shift]
                t = t if a == b else t + t
                total = t if total is None else total + t
        return total

    one = jnp.ones((8, 128), F32)
    zero = jnp.zeros((8, 128), F32)
    rho, pi = [one], [one]
    xs = [zero, zero, zero]
    norm = mu[0]
    for n in range(3):
        alpha = norm / quad(pi, 1)
        for a in range(n + 1):
            xs[a] = xs[a] + alpha * pi[a]
        moved = [zero] + [alpha * c for c in pi]
        rho = [(rho[a] if a < len(rho) else zero) - moved[a] for a in range(n + 2)]
        if n < 2:
            new = quad(rho, 0)
            beta = new / norm
            pi = [rho[a] + (beta * pi[a] if a < len(pi) else zero) for a in range(n + 2)]
            norm = new

    on_plane = 1.0 - pm
    for k in range(8):
        for j in range(8):
            t = tile(k, j)
            vel[t, :] = (rows(QB, 64 + k * 8 + j) * on_plane + xs[0] * V[0, t, :]
                         + xs[1] * V[1, t, :] + xs[2] * V[2, t, :])
            res[t, :] = (R0[t, :] + rho[1] * WA[0, t, :] + rho[2] * WA[1, t, :]
                         + rho[3] * WA[2, t, :])

    for d in range(-2, 3):
        when_there(d, lambda d=d: req_copy(d).wait_send())
    for d in (-1, 1):
        when_there(d, lambda d=d: aux_copy(d).wait_send())
        when_there(d, lambda d=d: face_copy(d).wait_send())
        when_there(d, lambda d=d: halo_copy(FB, 0, d).wait_send())
        when_there(d, lambda d=d: halo_copy(OUT, 3, d).wait_send())
    for f in range(5):
        for s in range(5):
            when_there(2 - s, lambda f=f, s=s: ans_copy(f, s).wait_send())

    def left(d, c):
        peer = lax.rem(q + d, NQ)
        pltpu.make_async_remote_copy(
            ar.at[q], ar.at[q], ar_s.at[d], ar_r.at[q],
            device_id=(m, peer), device_id_type=MESH).wait_send()
        return c

    lax.fori_loop(1, NQ, left, 0)


def body(donor_fields, interp_weights, donor_owner, donor_element, geometry, wall_flag, forcing):
    vm = pl.BlockSpec(memory_space=pltpu.VMEM)
    hbm = pl.BlockSpec(memory_space=pl.ANY)
    dma = pltpu.SemaphoreType.DMA
    f32 = lambda *shape: pltpu.VMEM(shape, F32)
    return pl.pallas_call(
        kernel,
        out_shape=(
            jax.ShapeDtypeStruct((512, 128), F32),
            jax.ShapeDtypeStruct((512, 128), F32),
            jax.ShapeDtypeStruct((5, 2048), F32),
        ),
        in_specs=[hbm, vm, vm, vm, vm, vm, hbm, vm],
        out_specs=(vm, vm, vm),
        scratch_shapes=[
            f32(5, 512, 128), f32(512, 128), f32(64, 128), f32(5, 64, 128),
            f32(8, 128), f32(2, 8, 128), f32(24 * NB, 128), pltpu.VMEM((NB, 128), jnp.int32),
            f32(5, NB, 128), f32(5, 5, 16, 128),
            f32(512, 128), f32(512, 128), f32(512, 128), f32(512, 128),
            f32(3, 512, 128), f32(3, 512, 128), f32(512, 128), f32(128, 128), f32(128, 128),
            f32(2, 8, 128), f32(2, 8, 128), f32(4, 2, 64, 128), f32(NQ, 1, 128),
            dma((2,)), dma((5,)), dma((5,)), dma((2,)), dma((2,)), dma((5, 5)), dma((5, 5)),
            dma((2,)), dma((2,)), dma((4, 2)), dma((4, 2)), dma((NQ,)), dma((NQ,)),
        ],
        compiler_params=pltpu.CompilerParams(
            collective_id=0, has_side_effects=True, vmem_limit_bytes=32 * 1024 * 1024),
        name="step_window",
    )(
        donor_fields, interp_weights, donor_owner.reshape(16, 128),
        donor_element.reshape(16, 128), geometry, wall_flag, forcing,
        jnp.asarray(const_table()),
    )


def solution(mesh):
    both = ("mesh", "dom")
    in_specs = (
        P(None, None, both), P(None, None, both), P(both, None), P(both),
        P(None, both), P(None, both), P(None, both),
    )
    out_specs = (P(None, both), P(None, both), P(None, both))
    return jax.shard_map(body, mesh=mesh, in_specs=in_specs, out_specs=out_specs, check_vma=False)
```

time: 539 us -> 68.8 us (0.13); the launches traced: 529 us -> 68.4 us
  local copies, waits for them, and re-layouts: 189 us -> 8.77 us
  other arithmetic: 141 us -> 0 us
  starting transfers between devices: 62.1 us -> 0 us
  blocking collectives: 59.2 us -> 0 us
  Pallas kernels: 0 us -> 59 us
  waiting for transfers between devices: 55.5 us -> 0 us
  between operations: 11.5 us -> 0.66 us
  matrix products: 10.3 us -> 0 us
    gather x8 -> x0, local copies, waits for them, and re-layouts: 93.9 us -> none  [the longest x5 68 us: body(): jnp.take(donor_fields, lookups, axis=2).reshape(field_count, 64, 8, count)]
    select_n x24 -> x0, other arithmetic: 80.6 us -> none  [the longest x5 61.5 us: body(): jnp.take(donor_fields, lookups, axis=2).reshape(field_count, 64, 8, count)]
    select_n x6 -> x0, local copies, waits for them, and re-layouts: 75.1 us -> none  [the longest x5 73.3 us: body(): jnp.take(donor_fields, lookups, axis=2).reshape(field_count, 64, 8, count)]
    all_to_all x2 -> x0, blocking collectives: 59.2 us -> none  [from_everyone(): lax.all_to_all(jnp.broadcast_to(value[None], (length, *value.shape)), axi...]
    pallas_call x0 -> x1, Pallas kernels: none -> 59 us  [body(): pl.pallas_call(kernel, out_shape=(jax.ShapeDtypeStruct((512, 128), F32),...]
    ppermute x20 -> x0, starting transfers between devices: 49.5 us -> none  [the longest x8 24.5 us: from_behind(): lax.ppermute(value, axis, [(source, source + steps) for source in range(l...]
    ppermute x20 -> x0, waiting for transfers between devices: 46.8 us -> none  [the longest x5 25.8 us: with_halo(): after = lax.ppermute(leading, axis, down)]
    reduce_sum x22 -> x0, other arithmetic: 44.8 us -> none  [the longest x5 39.1 us: body(): jnp.sum(gathered * piece[0:8][None, None], axis=2)]
  transfers between devices with their start and end apart: 21 -> 0, of which waited for: 15 -> 0; matrix products, arithmetic and copies ran while one was open for 40% -> 0% of each run, Pallas kernels for 0% -> 0%
where the time goes in v1:
time: 68.8 us; the launch traced here: 68.4 us
  Pallas kernels  59 us (86%)
  local copies, waits for them, and re-layouts  8.77 us (13%)
    pallas_call x1, Pallas kernels, body(): pl.pallas_call(kernel, out_shape=(jax.ShapeDtypeStruct((512, 128), F32),...  59 us
    unnamed x19, local copies, waits for them, and re-layouts  8.77 us

profile of v1, /device:TPU:0, one launch (start us, length us, event | category | flops | bytes accessed | tf_op | source)
XLA Modules:
  0.0 68.4 jit_solution(366283308088980315)
XLA Ops:
  0.6 0.0 copy-start
  0.6 1.3 %copy-done = f32[5,512,128]{2,1,0:T(8,128)S(1)} copy-done((f32[5,512,128]{2,1,0:T(8,128)S(1)}, f32[5,512,128]{2,1,0:T(8,128)}, u32[]{:S(2)}) %copy-start) | copy-done | bytes 1310744
  1.9 0.0 copy-start.1
  2.0 0.9 %copy-done.1 = f32[512,128]{1,0:T(8,128)S(1)} copy-done((f32[512,128]{1,0:T(8,128)S(1)}, f32[512,128]{1,0:T(8,128)}, u32[]{:S(2)}) %copy-start.1) | copy-done | bytes 262168
  2.9 0.0 copy-start.2
  2.9 0.9 %copy-done.2 = f32[3,8,2048]{2,1,0:T(8,128)S(1)} copy-done((f32[3,8,2048]{2,1,0:T(8,128)S(1)}, f32[3,8,2048]{2,1,0:T(8,128)}, u32[]{:S(2)}) %copy-start.2) | copy-done | bytes 196632
  3.8 0.0 copy-start.3
  3.8 0.8 %copy-done.3 = f32[96,128]{1,0:T(8,128)S(1)} copy-done((f32[96,128]{1,0:T(8,128)S(1)}, f32[96,128]{1,0:T(8,128)}, u32[]{:S(2)}) %copy-start.3) | copy-done | bytes 49176
  4.6 0.0 copy-start.4
  4.6 0.7 %copy-done.4 = s32[2048,1]{0,1:T(1,128)S(1)} copy-done((s32[2048,1]{0,1:T(1,128)S(1)}, s32[2048,1]{0,1:T(1,128)}, u32[]{:S(2)}) %copy-start.4) | copy-done | bytes 8216
  5.3 0.0 copy-start.5
  5.3 0.7 %copy-done.5 = s32[2048]{0:T(1024)S(1)} copy-done((s32[2048]{0:T(1024)S(1)}, s32[2048]{0:T(1024)}, u32[]{:S(2)}) %copy-start.5) | copy-done | bytes 8216
  6.0 0.0 copy-start.6
  6.0 0.7 copy-done.6
  6.7 0.0 copy-start.7
  6.7 0.7 copy-done.7
  7.4 59.0 %step_window.1 = (f32[512,128]{1,0:T(8,128)S(1)}, f32[512,128]{1,0:T(8,128)S(1)}, f32[5,2048]{1,0:T(8,128)S(1)}) custom-call(f32[5,512,128]{2,1,0:T(8,128)S(1)} %copy-done, f32[3,8,2048]{2,1,0:T(8,128)S(1)} %copy-done.2, s32[16,128]{1,0:T(8,128)S(1)} %bitcast.2, s32[16,128]{1,0:T(8,128)S(1)} %bitcast.3, f32[4,128]{1,0:T(4,128)S(1)} %copy-done.6, ...), custom_call_target="tpu_custom_call" | custom-call | tf_op jit(solution)/shard_map/step_window/pallas_call | solution.py:584
  66.4 0.7 %copy.14 = f32[512,128]{1,0:T(8,128)} copy(f32[512,128]{1,0:T(8,128)S(1)} %get-tuple-element.6) | data formatting | bytes 524288
  67.1 0.7 %copy.15 = f32[512,128]{1,0:T(8,128)} copy(f32[512,128]{1,0:T(8,128)S(1)} %get-tuple-element.7) | data formatting | bytes 524288
  67.8 0.6 copy.16
Async XLA Ops:
  0.6 1.3 %copy-start = (f32[5,512,128]{2,1,0:T(8,128)S(1)}, f32[5,512,128]{2,1,0:T(8,128)}, u32[]{:S(2)}) copy-start(f32[5,512,128]{2,1,0:T(8,128)} %donor_hbm.1) | copy-start | bytes 3932164
  1.9 0.9 %copy-start.1 = (f32[512,128]{1,0:T(8,128)S(1)}, f32[512,128]{1,0:T(8,128)}, u32[]{:S(2)}) copy-start(f32[512,128]{1,0:T(8,128)} %forc_hbm.1) | copy-start | bytes 786436
  2.9 0.9 %copy-start.2 = (f32[3,8,2048]{2,1,0:T(8,128)S(1)}, f32[3,8,2048]{2,1,0:T(8,128)}, u32[]{:S(2)}) copy-start(f32[3,8,2048]{2,1,0:T(8,128)} %wts.1) | copy-start | bytes 589828
  3.8 0.8 %copy-start.3 = (f32[96,128]{1,0:T(8,128)S(1)}, f32[96,128]{1,0:T(8,128)}, u32[]{:S(2)}) copy-start(f32[96,128]{1,0:T(8,128)} %constant.2.clone.ct) | copy-start | bytes 147460
  4.6 0.7 %copy-start.4 = (s32[2048,1]{0,1:T(1,128)S(1)}, s32[2048,1]{0,1:T(1,128)}, u32[]{:S(2)}) copy-start(s32[2048,1]{0,1:T(1,128)} %param.10) | copy-start | bytes 24580
  5.3 0.7 %copy-start.5 = (s32[2048]{0:T(1024)S(1)}, s32[2048]{0:T(1024)}, u32[]{:S(2)}) copy-start(s32[2048]{0:T(1024)} %param.11) | copy-start | bytes 24580
  6.0 0.7 copy-start.6
  6.7 0.7 copy-start.7

commit v2 on v1

--- a/solution.py
+++ b/solution.py
@@ -12,6 +12,9 @@
 F32 = jnp.float32
 NQ = 64
 NB = 80
+KM = 6
+HALF = KM * 64
+BF16 = jnp.bfloat16
 
 
 def legendre_pair(values, degree):
@@ -68,11 +71,12 @@
 
 
 def kernel(
-    donor_hbm, wts, owner, elem, geo, wall, forc_hbm, ct,
+    donor_hbm, wts_hbm, owner_hbm, elem_hbm, geo_hbm, wall_hbm, forc_hbm, ct_hbm,
     vel, res, iv,
-    donor, forc, req_src, req, aux_src, aux, W, IDX, ans_src, ans,
-    FB, OUT, R0, INV, V, WA, DG, ND, QB, face_src, face, halo, ar,
-    in_sem, req_s, req_r, aux_s, aux_r, ans_s, ans_r, face_s, face_r, halo_s, halo_r, ar_s, ar_r,
+    donor, wts, owner, elem, geo, wall, forc, ct, nat, req_src, req, aux_src, aux, W, IDX, OH, DB,
+    ans_src, ans, fbuf, nbf, got,
+    FB, OUT, R0, INV, V, WA, DG, ND, QB, halo, ar,
+    in_sem, req_s, req_r, aux_s, aux_r, ans_s, ans_r, nb_s, nb_r, halo_s, halo_r, ar_s, ar_r,
 ):
     m = lax.axis_index("mesh")
     q = lax.axis_index("dom")
@@ -82,11 +86,16 @@
     def there(d):
         return jnp.logical_and(q + d >= 0, q + d < NQ)
 
+    pairs = ((wts_hbm, wts), (ct_hbm, ct), (owner_hbm, owner), (elem_hbm, elem), (geo_hbm, geo),
+             (wall_hbm, wall), (forc_hbm, forc), (donor_hbm, donor))
+    loads = [pltpu.make_async_copy(a, b, in_sem.at[n]) for n, (a, b) in enumerate(pairs)]
+    for load in loads:
+        load.start()
+
     for d, s in ((-1, 0), (1, 1)):
         @pl.when(jnp.logical_not(there(d)))
         def _(s=s):
             aux[s] = jnp.zeros((8, 128), F32)
-            face[s] = jnp.zeros((8, 128), F32)
             for r in range(4):
                 halo[r, s] = jnp.zeros((64, 128), F32)
     for d in (-2, -1, 1, 2):
@@ -95,18 +104,23 @@
             req[2 - d] = jnp.zeros((64, 128), F32)
             ans[2 + d] = jnp.zeros((5, 16, 128), F32)
 
-    in_donor = pltpu.make_async_copy(donor_hbm, donor, in_sem.at[0])
-    in_forc = pltpu.make_async_copy(forc_hbm, forc, in_sem.at[1])
-    in_forc.start()
-    in_donor.start()
+    def hears(side, s):
+        r = 2 * side - 1
+        return jnp.logical_and(there(r), there(r + s - 2))
+
+    for side in range(2):
+        for s in range(5):
+            @pl.when(jnp.logical_not(hears(side, s)))
+            def _(side=side, s=s):
+                nbf[side, s] = jnp.zeros((2, 1, 128), F32)
 
     def greet(d, c):
         peer = lax.rem(q + d, NQ)
         pl.semaphore_signal(barrier, inc=1, device_id=(m, peer), device_id_type=MESH)
         return c
 
-    lax.fori_loop(1, NQ, greet, 0)
-    for d in range(-2, 3):
+    lax.fori_loop(1, NQ, greet, 0, unroll=9)
+    for d in range(-3, 4):
         @pl.when(there(d))
         def _(d=d):
             pl.semaphore_signal(barrier, inc=1, device_id=(om, q + d), device_id_type=MESH)
@@ -115,23 +129,35 @@
     lane = lax.broadcasted_iota(jnp.int32, (8, 128), 1)
     xl = lane & 7
     yl = lane >> 3
+    for load in loads[:6]:
+        load.wait()
     xcol = ct[0:8, :]
     wcol = ct[8:16, :]
 
     for d in range(3):
         for b in range(16):
             t = wts[d, :, b * 128 : (b + 1) * 128] * xcol
-            req_src[d * 16 + b : d * 16 + b + 1, :] = jnp.sum(t, axis=0, keepdims=True)
-    req_src[48:64, :] = (owner[...] * 128 + elem[...]).astype(F32)
+            nat[d * 16 + b : d * 16 + b + 1, :] = jnp.sum(t, axis=0, keepdims=True)
+    nat[48:64, :] = (owner[...] * 128 + elem[...]).astype(F32)
+
+    def lanes(value, at):
+        return jnp.take_along_axis(value, at, axis=1, mode="promise_in_bounds")
+
+    from_y = lane >> 4 == i0
+    for d in range(4):
+        for s in range(2):
+            a = nat[d * 16 + s * 8 : d * 16 + s * 8 + 8, :]
+            for k in range(8):
+                t = lanes(a, ((lane >> 3) & 1) * 64 + k * 8 + (lane & 7))
+                at = d * 16 + k * 2 + s
+                req_src[at : at + 1, :] = jnp.sum(
+                    jnp.where(from_y, t, 0.0), axis=0, keepdims=True)
     aux_src[0:4, :] = geo[...]
     aux_src[4:6, :] = jnp.dot(
         wall[...].astype(F32), ct[88:96, :], preferred_element_type=F32
     )
     aux_src[6:8, :] = jnp.zeros((2, 128), F32)
 
-    width = sum(there(d).astype(jnp.int32) for d in range(-2, 3))
-    pl.semaphore_wait(barrier, NQ - 1 + width)
-
     def req_copy(d):
         return pltpu.make_async_remote_copy(
             req_src, req.at[d + 2], req_s.at[d + 2], req_r.at[d + 2],
@@ -143,33 +169,31 @@
             aux_src, aux.at[1 - s], aux_s.at[s], aux_r.at[1 - s],
             device_id=(m, q + d), device_id_type=MESH)
 
-    def face_copy(d):
-        s = (d + 1) // 2
-        return pltpu.make_async_remote_copy(
-            face_src.at[s], face.at[1 - s], face_s.at[s], face_r.at[1 - s],
-            device_id=(m, q + d), device_id_type=MESH)
-
     def halo_copy(src, r, d):
         s = (d + 1) // 2
         return pltpu.make_async_remote_copy(
             src.at[pl.ds(s * 448, 64)], halo.at[r, 1 - s], halo_s.at[r, s], halo_r.at[r, 1 - s],
             device_id=(m, q + d), device_id_type=MESH)
 
+    def near_copy(s, side):
+        return pltpu.make_async_remote_copy(
+            fbuf.at[s, side], nbf.at[1 - side, s], nb_s.at[s, side], nb_r.at[1 - side, s],
+            device_id=(om, q + 1 - s + 2 * side), device_id_type=MESH)
+
+    def tells(s, side):
+        return jnp.logical_and(there(2 - s), there(1 - s + 2 * side))
+
     def ans_copy(f, s):
         d = 2 - s
+        at = s * 16 if isinstance(s, int) else pl.multiple_of(s * 16, 16)
         return pltpu.make_async_remote_copy(
-            ans_src.at[f, pl.ds(s * 16, 16)], ans.at[s, f], ans_s.at[f, s], ans_r.at[f, s],
+            ans_src.at[f, pl.ds(at, 16)], ans.at[s, f], ans_s.at[f, s], ans_r.at[f, s],
             device_id=(om, q + d), device_id_type=MESH)
 
     def when_there(d, act):
         @pl.when(there(d))
         def _():
             act()
-
-    for d in (2, -2, 1, -1, 0):
-        when_there(d, lambda d=d: req_copy(d).start())
-    for d in (-1, 1):
-        when_there(d, lambda d=d: aux_copy(d).start())
 
     m7x = jnp.logical_and(i0 == 7, xl < 7)
     m0x = jnp.logical_and(i0 == 0, xl > 0)
@@ -205,15 +229,41 @@
     def wkj(k, j):
         return float(WQ[k] * WQ[j])
 
-    in_forc.wait()
+    loads[6].wait()
     g3w = g3 * wcol
     for k in range(8):
         for j in range(8):
             FB[tile(k, j), :] = forc[tile(k, j), :] * (g3w * wkj(k, j))
     sum_xy(FB, 0, 8)
+
+    kdiag = ct[16:24, :]
+
+    def diag_tile(h0, h1, h2, h3, k, j):
+        return (h0 * kdiag + h1 * float(KP[j, j]) + h2 * float(KP[k, k]) + h3) * (
+            wcol * wkj(k, j))
+
+    for k in range(8):
+        for j in range(8):
+            DG[tile(k, j), :] = diag_tile(g0, g1, g2, g3, k, j)
+    sum_xy(DG, 0, 8)
+
+    loads[7].wait()
+    for f in range(5):
+        for at in range(0, HALF, 64):
+            value = donor[f, at : at + 64, :]
+            high = value.astype(BF16)
+            DB[f * HALF + at : f * HALF + at + 64, 0:128] = high
+            DB[f * HALF + at : f * HALF + at + 64, 128:256] = (
+                value - high.astype(F32)).astype(BF16)
+
+    width = sum(there(d).astype(jnp.int32) for d in range(-3, 4))
+    pl.semaphore_wait(barrier, NQ - 1 + width)
+    for d in (2, -2, 1, -1, 0):
+        when_there(d, lambda d=d: req_copy(d).start())
+    for d in (-1, 1):
+        when_there(d, lambda d=d: aux_copy(d).start())
     for d in (-1, 1):
         when_there(d, lambda d=d: halo_copy(FB, 0, d).start())
-
     for d, s in ((-1, 0), (1, 1)):
         when_there(d, lambda d=d, s=s: aux_copy(-d).wait_recv())
 
@@ -238,20 +288,10 @@
             return pm
         return masks[j, "lo" if k == 0 else "hi" if k == 7 else "in"]
 
-    kdiag = ct[16:24, :]
-
-    def diag_tile(h0, h1, h2, h3, k, j):
-        return (h0 * kdiag + h1 * float(KP[j, j]) + h2 * float(KP[k, k]) + h3) * (
-            wcol * wkj(k, j))
-
-    for k in range(8):
-        for j in range(8):
-            DG[tile(k, j), :] = diag_tile(g0, g1, g2, g3, k, j)
     for s in range(2):
         h = [jnp.broadcast_to(aux[s, n : n + 1, :], (8, 128)) for n in range(4)]
         for j in range(8):
             ND[s * 64 + j * 8 : s * 64 + j * 8 + 8, :] = diag_tile(*h, 0, j)
-    sum_xy(DG, 0, 8)
     sum_xy(ND, 0, 2)
     for k in range(8):
         for j in range(8):
@@ -262,14 +302,14 @@
                 value = value + ND[tile(1, j), :]
             INV[tile(k, j), :] = free(k, j) / value
 
-    in_donor.wait()
+    row_of = lax.broadcasted_iota(jnp.int32, (128, 128), 0)
 
     def weights(s):
         for h in range(2):
             at = s * 16 + 8 * h
             code = req[s, 48 + 8 * h : 56 + 8 * h, :] - (q * 128).astype(F32)
             mine = jnp.logical_and(code >= 0.0, code < 128.0)
-            IDX[at : at + 8, :] = jnp.where(mine, code, 0.0).astype(jnp.int32)
+            IDX[pl.ds(pl.multiple_of(at, 8), 8), :] = jnp.where(mine, code, 0.0).astype(jnp.int32)
             keep = jnp.where(mine, 1.0, 0.0)
             for d in range(3):
                 xi = req[s, d * 16 + 8 * h : d * 16 + 8 * h + 8, :]
@@ -284,72 +324,88 @@
                     a = a * float(LC[n])
                     if d == 0:
                         a = a * keep
-                    W[(d * 8 + n) * NB + at : (d * 8 + n) * NB + at + 8, :] = a
-
-    def evaluate(f, first, count, unroll):
-        def block(b):
-            idx = jnp.broadcast_to(IDX[pl.ds(b, 1), :], (8, 128))
-            wi = W[pl.ds(b, 8, stride=NB), :]
-            total = None
-            for k in range(8):
-                wk = jnp.broadcast_to(W[pl.ds((16 + k) * NB + b, 1), :], (8, 128))
-                part = None
-                for j in range(8):
-                    wj = jnp.broadcast_to(W[pl.ds((8 + j) * NB + b, 1), :], (8, 128))
-                    g = jnp.take_along_axis(
-                        donor[f, tile(k, j), :], idx, axis=1, mode="promise_in_bounds")
-                    part = g * wj if part is None else part + g * wj
-                total = part * wk if total is None else total + part * wk
-            ans_src[f, pl.ds(b, 1), :] = jnp.sum(total * wi, axis=0, keepdims=True)
-
-        def step(n, c):
-            for u in range(unroll):
-                block(first + n * unroll + u)
+                    W[pl.ds(pl.multiple_of((s * 24 + d * 8 + n) * 16 + 8 * h, 8), 8), :] = a
+        for u in range(16):
+            column = jnp.broadcast_to(IDX[pl.ds(s * 16 + u, 1), :], (128, 128))
+            OH[s, :, u * 128 : (u + 1) * 128] = jnp.where(
+                row_of == column, 1.0, 0.0).astype(BF16)
+
+    def evaluate(fields, s):
+        hot = OH[s]
+        hot = jnp.concatenate([hot, hot], axis=0)
+        picked = {}
+        for f in fields:
+            picked[f] = jnp.dot(DB[f * HALF : (f + 1) * HALF, :], hot, preferred_element_type=F32)
+        base = s * 384
+        for f in fields:
+            for u in range(16):
+                idx = jnp.broadcast_to(IDX[pl.ds(s * 16 + u, 1), :], (8, 128))
+                wi = W[pl.ds(base + u, 8, stride=16), :]
+                wj = [jnp.broadcast_to(W[pl.ds(base + (8 + j) * 16 + u, 1), :], (8, 128))
+                      for j in range(8)]
+                total = None
+                for k in range(8):
+                    wk = jnp.broadcast_to(W[pl.ds(base + (16 + k) * 16 + u, 1), :], (8, 128))
+                    part = None
+                    for j in range(8):
+                        t = tile(k, j)
+                        if k < KM:
+                            g = picked[f][t, u * 128 : (u + 1) * 128]
+                        else:
+                            g = lanes(donor[f, t, :], idx)
+                        part = g * wj[j] if part is None else part + g * wj[j]
+                    total = part * wk if total is None else total + part * wk
+                line = jnp.sum(total * wi, axis=0, keepdims=True)
+                ans_src[f, pl.ds(s * 16 + u, 1), :] = line
+                if f == 0 and u in (0, 1, 14, 15):
+                    fbuf[s, u // 14, u % 2] = line
+
+    def all_slots(fields):
+        def step(s, c):
+            evaluate(fields, s)
             return c
 
-        lax.fori_loop(0, count // unroll, step, 0)
-
-    def send_field(f):
-        for s in (0, 4, 1, 3, 2):
-            when_there(2 - s, lambda s=s: ans_copy(f, s).start())
-
-    for s in (2, 1, 3, 0, 4):
-        when_there(2 - s, lambda s=s: req_copy(s - 2).wait_recv())
+        lax.fori_loop(0, 5, step, 0)
+        for f in fields:
+            for s in (0, 4, 1, 3, 2):
+                when_there(2 - s, lambda f=f, s=s: ans_copy(f, s).start())
+
+    def serve(n, c):
+        s = 2 + ((n + 1) // 2) * (1 - 2 * (n % 2))
+        when_there(2 - s, lambda: req_copy(s - 2).wait_recv())
         weights(s)
-        evaluate(0, s * 16, 16, 8)
-        when_there(2 - s, lambda s=s: ans_copy(0, s).start())
-
-    evaluate(1, 0, NB, 8)
-    send_field(1)
+        evaluate((0,), s)
+        when_there(2 - s, lambda: ans_copy(0, s).start())
+        for side in range(2):
+            @pl.when(tells(s, side))
+            def _(side=side):
+                near_copy(s, side).start()
+        return c
+
+    lax.fori_loop(0, 5, serve, 0)
+    all_slots((1, 2))
 
     for s in range(5):
         when_there(s - 2, lambda s=s: ans_copy(0, s).wait_recv())
-    got = ans[0, 0] + ans[1, 0] + ans[2, 0] + ans[3, 0] + ans[4, 0]
-    turned = jnp.transpose(jnp.concatenate([got, jnp.zeros((112, 128), F32)], 0))
-    column = jnp.where(xl == 7, 8, 0) + (yl >> 1)
-    even = (yl & 1) == 0
-    ends = jnp.logical_or(xl == 0, xl == 7)
-    T = []
-    for k in range(8):
-        a = jnp.take_along_axis(turned[k * 8 : k * 8 + 8, :], column, axis=1,
-                                mode="promise_in_bounds")
-        b = jnp.take_along_axis(turned[64 + k * 8 : 72 + k * 8, :], column, axis=1,
-                                mode="promise_in_bounds")
-        t = jnp.where(ends, jnp.where(even, a, b), 0.0)
-        T.append(t + jnp.where(m7y, pltpu.roll(pltpu.roll(t, 120, axis=1), 7, axis=0), 0.0)
-                 + jnp.where(m0y, pltpu.roll(pltpu.roll(t, 8, axis=1), 1, axis=0), 0.0))
-    face_src[0] = T[0]
-    face_src[1] = T[7]
-    for d in (-1, 1):
-        when_there(d, lambda d=d: face_copy(d).start())
-
-    evaluate(2, 0, NB, 8)
-    send_field(2)
-
-    for d in (-1, 1):
-        when_there(d, lambda d=d: face_copy(-d).wait_recv())
-    T[0] = T[0] + face[0]
-    T[7] = T[7] + face[1]
+    for side in range(2):
+        for s in range(5):
+            @pl.when(hears(side, s))
+            def _(side=side, s=s):
+                near_copy(s, 1 - side).wait_recv()
+    got[...] = ans[0, 0] + ans[1, 0] + ans[2, 0] + ans[3, 0] + ans[4, 0]
+
+    def on_planes(low, high):
+        at = yl * 8 + i0
+        t = jnp.where(xl == 0, lanes(jnp.broadcast_to(low, (8, 128)), at),
+                      jnp.where(xl == 7, lanes(jnp.broadcast_to(high, (8, 128)), at), 0.0))
+        return (t + jnp.where(m7y, pltpu.roll(pltpu.roll(t, 120, axis=1), 7, axis=0), 0.0)
+                + jnp.where(m0y, pltpu.roll(pltpu.roll(t, 8, axis=1), 1, axis=0), 0.0))
+
+    T = [on_planes(got[2 * k : 2 * k + 1, :], got[2 * k + 1 : 2 * k + 2, :]) for k in range(8)]
+    for side, k in ((0, 0), (1, 7)):
+        low, high = (sum(nbf[side, s, n] for s in range(1, 5)) + nbf[side, 0, n]
+                     for n in range(2))
+        T[k] = T[k] + on_planes(low, high)
     czd = jnp.where(q > 0, 0.5, 1.0).astype(F32)
     czu = jnp.where(q < NQ - 1, 0.5, 1.0).astype(F32)
     cyv = jnp.where(jnp.logical_or(m7y, m0y), 0.5, 1.0)
@@ -462,15 +518,20 @@
 
         return product_sum(make)
 
+    row = [jnp.zeros((1, 128), F32), 0]
+    lane_of = lax.broadcasted_iota(jnp.int32, (1, 128), 1)
+
+    def collect():
+        while row[1] < len(moments):
+            t = jnp.sum(jnp.sum(moments[row[1]], axis=0, keepdims=True), axis=1, keepdims=True)
+            row[0] = jnp.where(lane_of == row[1], t, row[0])
+            row[1] += 1
+        return row[0]
+
     for n in range(3):
         moments.append(local_operator(V.at[n], OUT))
         if n == 2:
-            row = jnp.zeros((1, 128), F32)
-            one = lax.broadcasted_iota(jnp.int32, (1, 128), 1)
-            for at, t in enumerate(moments):
-                t = jnp.sum(jnp.sum(t, axis=0, keepdims=True), axis=1, keepdims=True)
-                row = jnp.where(one == at, t, row)
-            ar[q] = row
+            ar[q] = collect()
 
             def tell(d, c):
                 peer = lax.rem(q + d, NQ)
@@ -479,13 +540,13 @@
                     device_id=(m, peer), device_id_type=MESH).start()
                 return c
 
-            lax.fori_loop(1, NQ, tell, 0)
+            lax.fori_loop(1, NQ, tell, 0, unroll=9)
         sum_xy(OUT, 0, 8)
         for d in (-1, 1):
             when_there(d, lambda d=d: halo_copy(OUT, n + 1, d).start())
         if n < 2:
-            evaluate(3 + n, 0, NB, 8)
-            send_field(3 + n)
+            collect()
+            all_slots((3 + n,))
         wait_halo(OUT, n + 1)
         if n < 2:
             for d in (-1, 1):
@@ -497,10 +558,17 @@
     for f in range(1, 5):
         for s in range(5):
             when_there(s - 2, lambda f=f, s=s: ans_copy(f, s).wait_recv())
+    from_k = (lane >> 3) & 7 == i0
     for f in range(5):
-        t = ans[0, f] + ans[1, f] + ans[2, f] + ans[3, f] + ans[4, f]
-        for b in range(16):
-            iv[f : f + 1, b * 128 : (b + 1) * 128] = t[b : b + 1, :]
+        for s in range(2):
+            a = (ans[0, f, pl.ds(s, 8, stride=2), :] + ans[1, f, pl.ds(s, 8, stride=2), :]
+                 + ans[2, f, pl.ds(s, 8, stride=2), :] + ans[3, f, pl.ds(s, 8, stride=2), :]
+                 + ans[4, f, pl.ds(s, 8, stride=2), :])
+            for y in range(8):
+                t = lanes(a, y * 16 + (lane >> 6) * 8 + (lane & 7))
+                at = (s * 8 + y) * 128
+                iv[f : f + 1, at : at + 128] = jnp.sum(
+                    jnp.where(from_k, t, 0.0), axis=0, keepdims=True)
 
     def hear(d, c):
         peer = lax.rem(q + d, NQ)
@@ -509,7 +577,7 @@
             device_id=(m, peer), device_id_type=MESH).wait_recv()
         return c
 
-    lax.fori_loop(1, NQ, hear, 0)
+    lax.fori_loop(1, NQ, hear, 0, unroll=9)
     parts = [ar[n] for n in range(NQ)]
     while len(parts) > 1:
         parts = [parts[n] + parts[n + 1] for n in range(0, len(parts), 2)]
@@ -559,12 +627,17 @@
         when_there(d, lambda d=d: req_copy(d).wait_send())
     for d in (-1, 1):
         when_there(d, lambda d=d: aux_copy(d).wait_send())
-        when_there(d, lambda d=d: face_copy(d).wait_send())
         when_there(d, lambda d=d: halo_copy(FB, 0, d).wait_send())
         when_there(d, lambda d=d: halo_copy(OUT, 3, d).wait_send())
     for f in range(5):
         for s in range(5):
             when_there(2 - s, lambda f=f, s=s: ans_copy(f, s).wait_send())
+
+    for s in range(5):
+        for side in range(2):
+            @pl.when(tells(s, side))
+            def _(s=s, side=side):
+                near_copy(s, side).wait_send()
 
     def left(d, c):
         peer = lax.rem(q + d, NQ)
@@ -573,41 +646,61 @@
             device_id=(m, peer), device_id_type=MESH).wait_send()
         return c
 
-    lax.fori_loop(1, NQ, left, 0)
+    lax.fori_loop(1, NQ, left, 0, unroll=9)
+
+
+def write_out(vel, res, iv, vel_out, res_out, iv_out, sem):
+    copies = [pltpu.make_async_copy(a, b, sem.at[n])
+              for n, (a, b) in enumerate(((vel, vel_out), (res, res_out), (iv, iv_out)))]
+    for copy in copies:
+        copy.start()
+    for copy in copies:
+        copy.wait()
 
 
 def body(donor_fields, interp_weights, donor_owner, donor_element, geometry, wall_flag, forcing):
     vm = pl.BlockSpec(memory_space=pltpu.VMEM)
-    hbm = pl.BlockSpec(memory_space=pl.ANY)
+    hbm = pl.BlockSpec(memory_space=pltpu.HBM)
     dma = pltpu.SemaphoreType.DMA
     f32 = lambda *shape: pltpu.VMEM(shape, F32)
-    return pl.pallas_call(
+    held = pl.pallas_call(
         kernel,
         out_shape=(
             jax.ShapeDtypeStruct((512, 128), F32),
             jax.ShapeDtypeStruct((512, 128), F32),
             jax.ShapeDtypeStruct((5, 2048), F32),
         ),
-        in_specs=[hbm, vm, vm, vm, vm, vm, hbm, vm],
+        in_specs=[hbm] * 8,
         out_specs=(vm, vm, vm),
         scratch_shapes=[
-            f32(5, 512, 128), f32(512, 128), f32(64, 128), f32(5, 64, 128),
+            f32(5, 512, 128), f32(3, 8, 2048), pltpu.VMEM((16, 128), jnp.int32),
+            pltpu.VMEM((16, 128), jnp.int32), f32(4, 128), pltpu.VMEM((2, 8), jnp.int32),
+            f32(512, 128), f32(96, 128), f32(64, 128), f32(64, 128), f32(5, 64, 128),
             f32(8, 128), f32(2, 8, 128), f32(24 * NB, 128), pltpu.VMEM((NB, 128), jnp.int32),
-            f32(5, NB, 128), f32(5, 5, 16, 128),
+            pltpu.VMEM((5, 128, 2048), BF16), pltpu.VMEM((5 * HALF, 256), BF16),
+            f32(5, NB, 128), f32(5, 5, 16, 128), f32(5, 2, 2, 1, 128), f32(2, 5, 2, 1, 128), f32(16, 128),
             f32(512, 128), f32(512, 128), f32(512, 128), f32(512, 128),
             f32(3, 512, 128), f32(3, 512, 128), f32(512, 128), f32(128, 128), f32(128, 128),
-            f32(2, 8, 128), f32(2, 8, 128), f32(4, 2, 64, 128), f32(NQ, 1, 128),
-            dma((2,)), dma((5,)), dma((5,)), dma((2,)), dma((2,)), dma((5, 5)), dma((5, 5)),
-            dma((2,)), dma((2,)), dma((4, 2)), dma((4, 2)), dma((NQ,)), dma((NQ,)),
+            f32(4, 2, 64, 128), f32(NQ, 1, 128),
+            dma((8,)), dma((5,)), dma((5,)), dma((2,)), dma((2,)), dma((5, 5)), dma((5, 5)),
+            dma((5, 2)), dma((2, 5)), dma((4, 2)), dma((4, 2)), dma((NQ,)), dma((NQ,)),
         ],
         compiler_params=pltpu.CompilerParams(
-            collective_id=0, has_side_effects=True, vmem_limit_bytes=32 * 1024 * 1024),
+            collective_id=0, has_side_effects=True, vmem_limit_bytes=64500000),
         name="step_window",
     )(
         donor_fields, interp_weights, donor_owner.reshape(16, 128),
         donor_element.reshape(16, 128), geometry, wall_flag, forcing,
         jnp.asarray(const_table()),
     )
+    return pl.pallas_call(
+        write_out,
+        out_shape=tuple(jax.ShapeDtypeStruct(a.shape, F32) for a in held),
+        in_specs=[vm] * 3,
+        out_specs=(hbm,) * 3,
+        scratch_shapes=[dma((3,))],
+        name="write_out",
+    )(*held)
 
 
 def solution(mesh):

time: 68.8 us -> 48.2 us (0.70)
  Pallas kernels: 59 us -> 47.4 us
  local copies, waits for them, and re-layouts: 8.77 us -> 0 us
    pallas_call x1, Pallas kernels: 59 us -> 45.5 us  [body(): pl.pallas_call(kernel, out_shape=(jax.ShapeDtypeStruct((512, 128), F32),...]
    unnamed x19 -> x0, local copies, waits for them, and re-layouts: 8.77 us -> none
    pallas_call x0 -> x1, Pallas kernels: none -> 1.86 us  [body(): pl.pallas_call(write_out, out_shape=tuple((jax.ShapeDtypeStruct(a.shape,...]
where the time goes in v2:
time: 48.2 us; the launch traced here: 48 us
  Pallas kernels  47.4 us (98%)
  between operations  0.64 us (1%)
    pallas_call x1, Pallas kernels, body(): pl.pallas_call(kernel, out_shape=(jax.ShapeDtypeStruct((512, 128), F32),...  45.5 us
    pallas_call x1, Pallas kernels, body(): pl.pallas_call(write_out, out_shape=tuple((jax.ShapeDtypeStruct(a.shape,...  1.86 us

profile of v2, /device:TPU:0, one launch (start us, length us, event | category | flops | bytes accessed | tf_op | source)
XLA Modules:
  0.0 48.0 jit_solution(208023513323124419)
XLA Ops:
  0.6 45.5 %step_window.1 = (f32[512,128]{1,0:T(8,128)}, f32[512,128]{1,0:T(8,128)}, f32[5,2048]{1,0:T(8,128)}) custom-call(f32[5,512,128]{2,1,0:T(8,128)} %donor_hbm.1, f32[3,8,2048]{2,1,0:T(8,128)} %wts_hbm.1, s32[16,128]{1,0:T(8,128)} %bitcast.2, s32[16,128]{1,0:T(8,128)} %bitcast.3, f32[4,128]{1,0:T(4,128)} %geo_hbm.1, s32[2,8]{1,0:T(2,128)} %wall_hbm.1, ...), custom_call_target="tpu_custom_call" | custom-call | tf_op jit(solution)/shard_map/step_window/pallas_call | solution.py:666
  46.2 1.9 %write_out.1 = (f32[512,128]{1,0:T(8,128)}, f32[512,128]{1,0:T(8,128)}, f32[5,2048]{1,0:T(8,128)}) custom-call(f32[512,128]{1,0:T(8,128)} %get-tuple-element.6.vel, f32[512,128]{1,0:T(8,128)} %get-tuple-element.7.res, f32[5,2048]{1,0:T(8,128)} %get-tuple-element.8.iv), custom_call_target="tpu_custom_call" | custom-call | tf_op jit(solution)/shard_map/write_out/pallas_call | solution.py:696

commit v3 on v2

--- a/solution.py
+++ b/solution.py
@@ -75,7 +75,7 @@
     vel, res, iv,
     donor, wts, owner, elem, geo, wall, forc, ct, nat, req_src, req, aux_src, aux, W, IDX, OH, DB,
     ans_src, ans, fbuf, nbf, got,
-    FB, OUT, R0, INV, V, WA, DG, ND, QB, halo, ar,
+    FB, OUT, INV, V, SB, DG, ND, QB, halo, ar,
     in_sem, req_s, req_r, aux_s, aux_r, ans_s, ans_r, nb_s, nb_r, halo_s, halo_r, ar_s, ar_r,
 ):
     m = lax.axis_index("mesh")
@@ -229,6 +229,15 @@
     def wkj(k, j):
         return float(WQ[k] * WQ[j])
 
+    loads[7].wait()
+    for f in range(1):
+        for at in range(0, HALF, 64):
+            value = donor[f, at : at + 64, :]
+            high = value.astype(BF16)
+            DB[f * HALF + at : f * HALF + at + 64, 0:128] = high
+            DB[f * HALF + at : f * HALF + at + 64, 128:256] = (
+                value - high.astype(F32)).astype(BF16)
+
     loads[6].wait()
     g3w = g3 * wcol
     for k in range(8):
@@ -236,6 +245,12 @@
             FB[tile(k, j), :] = forc[tile(k, j), :] * (g3w * wkj(k, j))
     sum_xy(FB, 0, 8)
 
+    width = sum(there(d).astype(jnp.int32) for d in range(-3, 4))
+    pl.semaphore_wait(barrier, NQ - 1 + width)
+    for d in (2, -2, 1, -1, 0):
+        when_there(d, lambda d=d: req_copy(d).start())
+    for d in (-1, 1):
+        when_there(d, lambda d=d: aux_copy(d).start())
     kdiag = ct[16:24, :]
 
     def diag_tile(h0, h1, h2, h3, k, j):
@@ -247,8 +262,7 @@
             DG[tile(k, j), :] = diag_tile(g0, g1, g2, g3, k, j)
     sum_xy(DG, 0, 8)
 
-    loads[7].wait()
-    for f in range(5):
+    for f in range(1, 5):
         for at in range(0, HALF, 64):
             value = donor[f, at : at + 64, :]
             high = value.astype(BF16)
@@ -256,17 +270,6 @@
             DB[f * HALF + at : f * HALF + at + 64, 128:256] = (
                 value - high.astype(F32)).astype(BF16)
 
-    width = sum(there(d).astype(jnp.int32) for d in range(-3, 4))
-    pl.semaphore_wait(barrier, NQ - 1 + width)
-    for d in (2, -2, 1, -1, 0):
-        when_there(d, lambda d=d: req_copy(d).start())
-    for d in (-1, 1):
-        when_there(d, lambda d=d: aux_copy(d).start())
-    for d in (-1, 1):
-        when_there(d, lambda d=d: halo_copy(FB, 0, d).start())
-    for d, s in ((-1, 0), (1, 1)):
-        when_there(d, lambda d=d, s=s: aux_copy(-d).wait_recv())
-
     plane = jnp.logical_or(
         jnp.logical_and(i0 == 0, xl == 0), jnp.logical_and(i0 == 7, xl == 7))
     pm = jnp.where(plane, 0.0, 1.0)
@@ -276,31 +279,24 @@
                 + jnp.where(m0x, pltpu.roll(row, 1, axis=1), 0.0))
 
     masks = {}
-    for n, (j, edge) in enumerate(((0, yl == 0), (7, yl == 15))):
-        own = wall_count(rows(aux_src, 4 + n))
-        below = wall_count(jnp.broadcast_to(aux[0, 4 + n : 5 + n, :], (8, 128)))
-        above = wall_count(jnp.broadcast_to(aux[1, 4 + n : 5 + n, :], (8, 128)))
-        for name, count in (("lo", own + below), ("in", own), ("hi", own + above)):
-            masks[j, name] = pm * (1.0 - jnp.where(edge, jnp.minimum(count, 1.0), 0.0))
+    edges = ((0, yl == 0), (7, yl == 15))
+
+    def wall_mask(j, name, count):
+        edge = edges[j // 7][1]
+        masks[j, name] = pm * (1.0 - jnp.where(edge, jnp.minimum(count, 1.0), 0.0))
+
+    own = [wall_count(rows(aux_src, 4 + n)) for n in range(2)]
+    for n in range(2):
+        wall_mask(7 * n, "in", own[n])
 
     def free(k, j):
         if j not in (0, 7):
             return pm
         return masks[j, "lo" if k == 0 else "hi" if k == 7 else "in"]
 
-    for s in range(2):
-        h = [jnp.broadcast_to(aux[s, n : n + 1, :], (8, 128)) for n in range(4)]
+    for k in range(1, 7):
         for j in range(8):
-            ND[s * 64 + j * 8 : s * 64 + j * 8 + 8, :] = diag_tile(*h, 0, j)
-    sum_xy(ND, 0, 2)
-    for k in range(8):
-        for j in range(8):
-            value = DG[tile(k, j), :]
-            if k == 0:
-                value = value + ND[tile(0, j), :]
-            if k == 7:
-                value = value + ND[tile(1, j), :]
-            INV[tile(k, j), :] = free(k, j) / value
+            INV[tile(k, j), :] = free(k, j) / DG[tile(k, j), :]
 
     row_of = lax.broadcasted_iota(jnp.int32, (128, 128), 0)
 
@@ -383,6 +379,26 @@
         return c
 
     lax.fori_loop(0, 5, serve, 0)
+    for d in (-1, 1):
+        when_there(d, lambda d=d: halo_copy(FB, 0, d).start())
+    for d, s in ((-1, 0), (1, 1)):
+        when_there(d, lambda d=d, s=s: aux_copy(-d).wait_recv())
+
+    for n in range(2):
+        for s, name in ((0, "lo"), (1, "hi")):
+            other = wall_count(jnp.broadcast_to(aux[s, 4 + n : 5 + n, :], (8, 128)))
+            wall_mask(7 * n, name, own[n] + other)
+
+    for s in range(2):
+        h = [jnp.broadcast_to(aux[s, n : n + 1, :], (8, 128)) for n in range(4)]
+        for j in range(8):
+            ND[s * 64 + j * 8 : s * 64 + j * 8 + 8, :] = diag_tile(*h, 0, j)
+    sum_xy(ND, 0, 2)
+    for k in (0, 7):
+        for j in range(8):
+            value = DG[tile(k, j), :] + ND[tile(k // 7, j), :]
+            INV[tile(k, j), :] = free(k, j) / value
+
     all_slots((1, 2))
 
     for s in range(5):
@@ -445,19 +461,24 @@
         for d in (-1, 1):
             when_there(d, lambda d=d: halo_copy(src, r, -d).wait_recv())
 
-    def product_sum(make):
-        total = None
-        for k in range(8):
-            part = None
+    def inner_sums(make, count, planes=range(8)):
+        totals = [None] * count
+        for k in planes:
+            parts = [None] * count
             for j in range(8):
-                t = make(k, j) * cxy.get(j, cx)
-                part = t if part is None else part + t
-            if k == 0:
-                part = part * czd
-            if k == 7:
-                part = part * czu
-            total = part if total is None else total + part
-        return total
+                one, others = make(k, j)
+                one = one * cxy.get(j, cx)
+                for n, other in enumerate(others):
+                    t = one * other
+                    parts[n] = t if parts[n] is None else parts[n] + t
+            for n in range(count):
+                t = parts[n]
+                if k == 0:
+                    t = t * czd
+                if k == 7:
+                    t = t * czu
+                totals[n] = t if totals[n] is None else totals[n] + t
+        return totals
 
     kxw = ct[80:88, :] * wcol
     wait_halo(FB, 0)
@@ -465,12 +486,12 @@
     def first(k, j):
         value = assembled(FB, 0, k, j) - rows(QB, k * 8 + j) * (kxw * wkj(k, j))
         value = value * free(k, j)
-        R0[tile(k, j), :] = value
+        SB[0, tile(k, j), :] = value
         pre = value * INV[tile(k, j), :]
         V[0, tile(k, j), :] = pre
-        return value * pre
-
-    moments = [product_sum(first)]
+        return pre, (value,)
+
+    moments = inner_sums(first, 1)
 
     kroll = [ct[16 + 8 * s : 24 + 8 * s, :] for s in range(8)]
 
@@ -487,14 +508,23 @@
             out[n], out[7 - n] = a + b, a - b
         return out
 
-    def local_operator(src, dst):
+    def ends_of_eight(v):
+        a, b = None, None
+        for c in range(4):
+            ta, tb = (v[c] + v[7 - c]) * float(KE[0, c]), (v[c] - v[7 - c]) * float(KO[0, c])
+            a = ta if a is None else a + ta
+            b = tb if b is None else b + tb
+        return {0: a + b, 7: a - b}
+
+    def local_operator(src, dst, planes, wanted):
+        faces = len(planes) == 2
         for j in range(8):
             v = [src[tile(k, j), :] for k in range(8)]
-            z = eight(v)
-            for k in range(8):
+            z = ends_of_eight(v) if faces else eight(v)
+            for k in planes:
                 dst[tile(k, j), :] = z[k] * g2 + v[k] * g3
         energy = None
-        for k in range(8):
+        for k in planes:
             v = [src[tile(k, j), :] for j in range(8)]
             y = eight(v)
             for j in range(8):
@@ -503,20 +533,21 @@
                     x = x + pltpu.roll(v[j], 8 - s, axis=0) * kroll[s]
                 value = (dst[tile(k, j), :] + y[j] * g1 + x * g0) * (wcol * wkj(k, j))
                 dst[tile(k, j), :] = value
-                t = v[j] * value
-                energy = t if energy is None else energy + t
+                if wanted:
+                    t = v[j] * value
+                    energy = t if energy is None else energy + t
         return energy
 
-    def fold(n):
+    def fold(n, planes):
         def make(k, j):
-            value = assembled(OUT, n + 1, k, j) * free(k, j)
-            WA[n, tile(k, j), :] = value
-            pre = value * INV[tile(k, j), :]
-            if n < 2:
-                V[n + 1, tile(k, j), :] = pre
-            return value * pre
-
-        return product_sum(make)
+            t = tile(k, j)
+            value = assembled(OUT, n + 1, k, j) * free(k, j) - SB[n, t, :]
+            SB[n + 1, t, :] = value
+            pre = value * INV[t, :]
+            V[n + 1, t, :] = pre
+            return pre, tuple(SB[a, t, :] for a in range(n + 1)) + (value,)
+
+        return inner_sums(make, n + 2, planes)
 
     row = [jnp.zeros((1, 128), F32), 0]
     lane_of = lax.broadcasted_iota(jnp.int32, (1, 128), 1)
@@ -528,32 +559,36 @@
             row[1] += 1
         return row[0]
 
-    for n in range(3):
-        moments.append(local_operator(V.at[n], OUT))
-        if n == 2:
-            ar[q] = collect()
-
-            def tell(d, c):
-                peer = lax.rem(q + d, NQ)
-                pltpu.make_async_remote_copy(
-                    ar.at[q], ar.at[q], ar_s.at[d], ar_r.at[q],
-                    device_id=(m, peer), device_id_type=MESH).start()
-                return c
-
-            lax.fori_loop(1, NQ, tell, 0, unroll=9)
-        sum_xy(OUT, 0, 8)
+    for n in range(2):
+        local_operator(V.at[n], OUT, (0, 7), False)
+        sum_xy(OUT, 0, 1)
+        sum_xy(OUT, 448, 1)
         for d in (-1, 1):
             when_there(d, lambda d=d: halo_copy(OUT, n + 1, d).start())
-        if n < 2:
-            collect()
-            all_slots((3 + n,))
+        local_operator(V.at[n], OUT, range(1, 7), False)
+        sum_xy(OUT, 64, 6)
+        inside = fold(n, range(1, 7))
+        collect()
+        all_slots((3 + n,))
         wait_halo(OUT, n + 1)
-        if n < 2:
-            for d in (-1, 1):
-                when_there(d, lambda d=d: halo_copy(OUT, n + 1, d).wait_send())
-            moments.append(fold(n))
-        else:
-            fold(n)
+        for d in (-1, 1):
+            when_there(d, lambda d=d: halo_copy(OUT, n + 1, d).wait_send())
+        moments.extend(a + b for a, b in zip(inside, fold(n, (0, 7))))
+
+    moments.append(local_operator(V.at[2], OUT, range(8), True))
+    ar[q] = collect()
+
+    def tell(d, c):
+        peer = lax.rem(q + d, NQ)
+        pltpu.make_async_remote_copy(
+            ar.at[q], ar.at[q], ar_s.at[d], ar_r.at[q],
+            device_id=(m, peer), device_id_type=MESH).start()
+        return c
+
+    lax.fori_loop(1, NQ, tell, 0, unroll=9)
+    sum_xy(OUT, 0, 8)
+    for d in (-1, 1):
+        when_there(d, lambda d=d: halo_copy(OUT, 3, d).start())
 
     for f in range(1, 5):
         for s in range(5):
@@ -570,6 +605,8 @@
                 iv[f : f + 1, at : at + 128] = jnp.sum(
                     jnp.where(from_k, t, 0.0), axis=0, keepdims=True)
 
+    wait_halo(OUT, 3)
+
     def hear(d, c):
         peer = lax.rem(q + d, NQ)
         pltpu.make_async_remote_copy(
@@ -585,14 +622,19 @@
     mu = [
         jnp.take_along_axis(sums, jnp.full((8, 128), n, jnp.int32), axis=1,
                             mode="promise_in_bounds")
-        for n in range(6)
+        for n in range(7)
     ]
 
-    def quad(c, shift):
+    gram = {(0, 0): mu[0], (0, 1): mu[1], (1, 1): mu[2], (0, 2): mu[3], (1, 2): mu[4],
+            (2, 2): mu[5]}
+    stiff = {(0, 0): mu[1] + mu[0], (0, 1): mu[2] + mu[1], (1, 1): mu[4] + mu[2],
+             (0, 2): mu[4] + mu[3], (1, 2): mu[5] + mu[4], (2, 2): mu[6]}
+
+    def quad(c, form):
         total = None
         for a in range(len(c)):
             for b in range(a, len(c)):
-                t = c[a] * c[b] * mu[a + b + shift]
+                t = c[a] * c[b] * form[a, b]
                 t = t if a == b else t + t
                 total = t if total is None else total + t
         return total
@@ -603,13 +645,14 @@
     xs = [zero, zero, zero]
     norm = mu[0]
     for n in range(3):
-        alpha = norm / quad(pi, 1)
+        alpha = norm / quad(pi, stiff)
         for a in range(n + 1):
             xs[a] = xs[a] + alpha * pi[a]
-        moved = [zero] + [alpha * c for c in pi]
+        moved = [(alpha * pi[a] if a <= n else zero) + (alpha * pi[a - 1] if a else zero)
+                 for a in range(n + 2)]
         rho = [(rho[a] if a < len(rho) else zero) - moved[a] for a in range(n + 2)]
         if n < 2:
-            new = quad(rho, 0)
+            new = quad(rho, gram)
             beta = new / norm
             pi = [rho[a] + (beta * pi[a] if a < len(pi) else zero) for a in range(n + 2)]
             norm = new
@@ -620,8 +663,9 @@
             t = tile(k, j)
             vel[t, :] = (rows(QB, 64 + k * 8 + j) * on_plane + xs[0] * V[0, t, :]
                          + xs[1] * V[1, t, :] + xs[2] * V[2, t, :])
-            res[t, :] = (R0[t, :] + rho[1] * WA[0, t, :] + rho[2] * WA[1, t, :]
-                         + rho[3] * WA[2, t, :])
+            image = assembled(OUT, 3, k, j) * free(k, j)
+            res[t, :] = (rho[0] * SB[0, t, :] + rho[1] * SB[1, t, :]
+                         + (rho[2] - rho[3]) * SB[2, t, :] + rho[3] * image)
 
     for d in range(-2, 3):
         when_there(d, lambda d=d: req_copy(d).wait_send())
@@ -679,7 +723,7 @@
             f32(8, 128), f32(2, 8, 128), f32(24 * NB, 128), pltpu.VMEM((NB, 128), jnp.int32),
             pltpu.VMEM((5, 128, 2048), BF16), pltpu.VMEM((5 * HALF, 256), BF16),
             f32(5, NB, 128), f32(5, 5, 16, 128), f32(5, 2, 2, 1, 128), f32(2, 5, 2, 1, 128), f32(16, 128),
-            f32(512, 128), f32(512, 128), f32(512, 128), f32(512, 128),
+            f32(512, 128), f32(512, 128), f32(512, 128),
             f32(3, 512, 128), f32(3, 512, 128), f32(512, 128), f32(128, 128), f32(128, 128),
             f32(4, 2, 64, 128), f32(NQ, 1, 128),
             dma((8,)), dma((5,)), dma((5,)), dma((2,)), dma((2,)), dma((5, 5)), dma((5, 5)),

time: 48.2 us -> 46 us (0.954)
  Pallas kernels: 47.4 us -> 45.2 us
    pallas_call x1, Pallas kernels: 45.5 us -> 43.3 us  [body(): pl.pallas_call(kernel, out_shape=(jax.ShapeDtypeStruct((512, 128), F32),...]
where the time goes in v3:
time: 46 us; the launch traced here: 45.8 us
  Pallas kernels  45.2 us (98%)
  between operations  0.64 us (1%)
    pallas_call x1, Pallas kernels, body(): pl.pallas_call(kernel, out_shape=(jax.ShapeDtypeStruct((512, 128), F32),...  43.3 us
    pallas_call x1, Pallas kernels, body(): pl.pallas_call(write_out, out_shape=tuple((jax.ShapeDtypeStruct(a.shape,...  1.86 us

profile of v3, /device:TPU:0, one launch (start us, length us, event | category | flops | bytes accessed | tf_op | source)
XLA Modules:
  0.0 45.8 jit_solution(1302649077229143341)
XLA Ops:
  0.6 43.3 %step_window.1 = (f32[512,128]{1,0:T(8,128)}, f32[512,128]{1,0:T(8,128)}, f32[5,2048]{1,0:T(8,128)}) custom-call(f32[5,512,128]{2,1,0:T(8,128)} %donor_hbm.1, f32[3,8,2048]{2,1,0:T(8,128)} %wts_hbm.1, s32[16,128]{1,0:T(8,128)} %bitcast.2, s32[16,128]{1,0:T(8,128)} %bitcast.3, f32[4,128]{1,0:T(4,128)} %geo_hbm.1, s32[2,8]{1,0:T(2,128)} %wall_hbm.1, ...), custom_call_target="tpu_custom_call" | custom-call | tf_op jit(solution)/shard_map/step_window/pallas_call | solution.py:710
  44.0 1.9 %write_out.1 = (f32[512,128]{1,0:T(8,128)}, f32[512,128]{1,0:T(8,128)}, f32[5,2048]{1,0:T(8,128)}) custom-call(f32[512,128]{1,0:T(8,128)} %get-tuple-element.6.vel, f32[512,128]{1,0:T(8,128)} %get-tuple-element.7.res, f32[5,2048]{1,0:T(8,128)} %get-tuple-element.8.iv), custom_call_target="tpu_custom_call" | custom-call | tf_op jit(solution)/shard_map/write_out/pallas_call | solution.py:740

commit v4 on v3

--- a/solution.py
+++ b/solution.py
@@ -72,10 +72,10 @@
 
 def kernel(
     donor_hbm, wts_hbm, owner_hbm, elem_hbm, geo_hbm, wall_hbm, forc_hbm, ct_hbm,
-    vel, res, iv,
+    vel_hbm, res_hbm, iv_hbm,
     donor, wts, owner, elem, geo, wall, forc, ct, nat, req_src, req, aux_src, aux, W, IDX, OH, DB,
     ans_src, ans, fbuf, nbf, got,
-    FB, OUT, INV, V, SB, DG, ND, QB, halo, ar,
+    FB, OUT, INV, V, SB, DG, ND, QB, halo, ar, vel, res, iv, out_sem,
     in_sem, req_s, req_r, aux_s, aux_r, ans_s, ans_r, nb_s, nb_r, halo_s, halo_r, ar_s, ar_r,
 ):
     m = lax.axis_index("mesh")
@@ -247,7 +247,7 @@
 
     width = sum(there(d).astype(jnp.int32) for d in range(-3, 4))
     pl.semaphore_wait(barrier, NQ - 1 + width)
-    for d in (2, -2, 1, -1, 0):
+    for d in (0, 1, -1, 2, -2):
         when_there(d, lambda d=d: req_copy(d).start())
     for d in (-1, 1):
         when_there(d, lambda d=d: aux_copy(d).start())
@@ -361,7 +361,7 @@
             evaluate(fields, s)
             return c
 
-        lax.fori_loop(0, 5, step, 0)
+        lax.fori_loop(0, 5, step, 0, unroll=5)
         for f in fields:
             for s in (0, 4, 1, 3, 2):
                 when_there(2 - s, lambda f=f, s=s: ans_copy(f, s).start())
@@ -605,6 +605,34 @@
                 iv[f : f + 1, at : at + 128] = jnp.sum(
                     jnp.where(from_k, t, 0.0), axis=0, keepdims=True)
 
+    outs = [pltpu.make_async_copy(iv, iv_hbm, out_sem.at[4])]
+    outs[0].start()
+
+    for d in range(-2, 3):
+        when_there(d, lambda d=d: req_copy(d).wait_send())
+    for d in (-1, 1):
+        when_there(d, lambda d=d: aux_copy(d).wait_send())
+        when_there(d, lambda d=d: halo_copy(FB, 0, d).wait_send())
+        when_there(d, lambda d=d: halo_copy(OUT, 3, d).wait_send())
+    for f in range(5):
+        for s in range(5):
+            when_there(2 - s, lambda f=f, s=s: ans_copy(f, s).wait_send())
+
+    for s in range(5):
+        for side in range(2):
+            @pl.when(tells(s, side))
+            def _(s=s, side=side):
+                near_copy(s, side).wait_send()
+
+    def left(d, c):
+        peer = lax.rem(q + d, NQ)
+        pltpu.make_async_remote_copy(
+            ar.at[q], ar.at[q], ar_s.at[d], ar_r.at[q],
+            device_id=(m, peer), device_id_type=MESH).wait_send()
+        return c
+
+    lax.fori_loop(1, NQ, left, 0, unroll=9)
+
     wait_halo(OUT, 3)
 
     def hear(d, c):
@@ -666,31 +694,13 @@
             image = assembled(OUT, 3, k, j) * free(k, j)
             res[t, :] = (rho[0] * SB[0, t, :] + rho[1] * SB[1, t, :]
                          + (rho[2] - rho[3]) * SB[2, t, :] + rho[3] * image)
-
-    for d in range(-2, 3):
-        when_there(d, lambda d=d: req_copy(d).wait_send())
-    for d in (-1, 1):
-        when_there(d, lambda d=d: aux_copy(d).wait_send())
-        when_there(d, lambda d=d: halo_copy(FB, 0, d).wait_send())
-        when_there(d, lambda d=d: halo_copy(OUT, 3, d).wait_send())
-    for f in range(5):
-        for s in range(5):
-            when_there(2 - s, lambda f=f, s=s: ans_copy(f, s).wait_send())
-
-    for s in range(5):
-        for side in range(2):
-            @pl.when(tells(s, side))
-            def _(s=s, side=side):
-                near_copy(s, side).wait_send()
-
-    def left(d, c):
-        peer = lax.rem(q + d, NQ)
-        pltpu.make_async_remote_copy(
-            ar.at[q], ar.at[q], ar_s.at[d], ar_r.at[q],
-            device_id=(m, peer), device_id_type=MESH).wait_send()
-        return c
-
-    lax.fori_loop(1, NQ, left, 0, unroll=9)
+        if k % 4 == 3:
+            at = pl.ds(k // 4 * 256, 256)
+            for n, (a, b) in enumerate(((vel, vel_hbm), (res, res_hbm))):
+                outs.append(pltpu.make_async_copy(a.at[at], b.at[at], out_sem.at[k // 4 * 2 + n]))
+                outs[-1].start()
+    for copy in outs:
+        copy.wait()
 
 
 def write_out(vel, res, iv, vel_out, res_out, iv_out, sem):
@@ -715,7 +725,7 @@
             jax.ShapeDtypeStruct((5, 2048), F32),
         ),
         in_specs=[hbm] * 8,
-        out_specs=(vm, vm, vm),
+        out_specs=(hbm, hbm, hbm),
         scratch_shapes=[
             f32(5, 512, 128), f32(3, 8, 2048), pltpu.VMEM((16, 128), jnp.int32),
             pltpu.VMEM((16, 128), jnp.int32), f32(4, 128), pltpu.VMEM((2, 8), jnp.int32),
@@ -725,7 +735,7 @@
             f32(5, NB, 128), f32(5, 5, 16, 128), f32(5, 2, 2, 1, 128), f32(2, 5, 2, 1, 128), f32(16, 128),
             f32(512, 128), f32(512, 128), f32(512, 128),
             f32(3, 512, 128), f32(3, 512, 128), f32(512, 128), f32(128, 128), f32(128, 128),
-            f32(4, 2, 64, 128), f32(NQ, 1, 128),
+            f32(4, 2, 64, 128), f32(NQ, 1, 128), f32(512, 128), f32(512, 128), f32(5, 2048), dma((5,)),
             dma((8,)), dma((5,)), dma((5,)), dma((2,)), dma((2,)), dma((5, 5)), dma((5, 5)),
             dma((5, 2)), dma((2, 5)), dma((4, 2)), dma((4, 2)), dma((NQ,)), dma((NQ,)),
         ],

time: 46 us -> 44.5 us (0.967)
  Pallas kernels: 45.2 us -> 43.7 us
    pallas_call x1, Pallas kernels: 43.3 us -> 41.9 us  [body(): pl.pallas_call(kernel, out_shape=(jax.ShapeDtypeStruct((512, 128), F32),...]
where the time goes in v4:
time: 44.5 us; the launch traced here: 44.4 us
  Pallas kernels  43.7 us (98%)
  between operations  0.64 us (1%)
    pallas_call x1, Pallas kernels, body(): pl.pallas_call(kernel, out_shape=(jax.ShapeDtypeStruct((512, 128), F32),...  41.9 us
    pallas_call x1, Pallas kernels, body(): pl.pallas_call(write_out, out_shape=tuple((jax.ShapeDtypeStruct(a.shape,...  1.86 us

profile of v4, /device:TPU:0, one launch (start us, length us, event | category | flops | bytes accessed | tf_op | source)
XLA Modules:
  0.0 44.4 jit_solution(17076150200142487344)
XLA Ops:
  0.6 41.9 %step_window.1 = (f32[512,128]{1,0:T(8,128)}, f32[512,128]{1,0:T(8,128)}, f32[5,2048]{1,0:T(8,128)}) custom-call(f32[5,512,128]{2,1,0:T(8,128)} %donor_hbm.1, f32[3,8,2048]{2,1,0:T(8,128)} %wts_hbm.1, s32[16,128]{1,0:T(8,128)} %bitcast.2, s32[16,128]{1,0:T(8,128)} %bitcast.3, f32[4,128]{1,0:T(4,128)} %geo_hbm.1, s32[2,8]{1,0:T(2,128)} %wall_hbm.1, ...), custom_call_target="tpu_custom_call" | custom-call | tf_op jit(solution)/shard_map/step_window/pallas_call | solution.py:720
  42.5 1.9 %write_out.1 = (f32[512,128]{1,0:T(8,128)}, f32[512,128]{1,0:T(8,128)}, f32[5,2048]{1,0:T(8,128)}) custom-call(f32[512,128]{1,0:T(8,128)} %get-tuple-element.6.vel, f32[512,128]{1,0:T(8,128)} %get-tuple-element.7.res, f32[5,2048]{1,0:T(8,128)} %get-tuple-element.8.iv), custom_call_target="tpu_custom_call" | custom-call | tf_op jit(solution)/shard_map/write_out/pallas_call | solution.py:750
